TPU v7x, 32 devices: a whole 2x2x4 slice. The times are simulated.
32 devices in a mesh: seq: 8 (over z, x), batch: 4 (over y, core).
Axes of the slice: x: 2, y: 2, z: 4, core: 2. Of those that a mesh axis runs over, the one named last changes fastest.
Arguments:
- tokens: bfloat16 [8, 1024, 768], P('batch', 'seq'), may hold values from -6 to 6
- cotangent: bfloat16 [8, 1024, 768], P('batch', 'seq'), may hold values from -6 to 6
- lengths: int32 [8], P('batch'), may hold values from 128 to 1024, as said below
- mixer_gain: bfloat16 [768], P(('seq', 'batch')), may hold values from 0.5 to 1.5
- mixer_inputs: bfloat16 [768, 2304], P(('seq', 'batch')), may hold values from -0.21875 to 0.21875
- shift_taps: bfloat16 [768, 4], P(('seq', 'batch')), may hold values from -3 to 3
- decay_rate: bfloat16 [768, 64], P(('seq', 'batch')), may hold values from 9.765625e-05 to 0.5
- state_in: bfloat16 [768, 64], P(('seq', 'batch')), may hold values from -3 to 3
- state_out: bfloat16 [768, 64], P(('seq', 'batch')), may hold values from -0.75 to 0.75
- state_skip: bfloat16 [768], P(('seq', 'batch')), may hold values from -4 to 4
- mixer_output: bfloat16 [768, 768], P(('seq', 'batch')), may hold values from -0.21875 to 0.21875
- first_gain: bfloat16 [768], P(('seq', 'batch')), may hold values from 0.5 to 1.5
- first_up: bfloat16 [768, 3072], P(('seq', 'batch')), may hold values from -0.21875 to 0.21875
- first_down: bfloat16 [3072, 768], P(('seq', 'batch')), may hold values from -0.109375 to 0.109375
- attend_gain: bfloat16 [768], P(('seq', 'batch')), may hold values from 0.5 to 1.5
- attend_inputs: bfloat16 [768, 2304], P(('seq', 'batch')), may hold values from -0.21875 to 0.21875
- attend_output: bfloat16 [768, 768], P(('seq', 'batch')), may hold values from -1.75 to 1.75
- second_gain: bfloat16 [768], P(('seq', 'batch')), may hold values from 0.5 to 1.5
- second_up: bfloat16 [768, 3072], P(('seq', 'batch')), may hold values from -0.21875 to 0.21875
- second_down: bfloat16 [3072, 768], P(('seq', 'batch')), may hold values from -0.109375 to 0.109375
Outputs:
- mixed: bfloat16 [8, 1024, 768], P('batch', 'seq')
- tokens_gradient: bfloat16 [8, 1024, 768], P('batch', 'seq')
- mixer_gain_gradient: float32 [768], P(('seq', 'batch'))
- mixer_inputs_gradient: float32 [768, 2304], P(('seq', 'batch'))
- shift_taps_gradient: float32 [768, 4], P(('seq', 'batch'))
- decay_rate_gradient: float32 [768, 64], P(('seq', 'batch'))
- state_in_gradient: float32 [768, 64], P(('seq', 'batch'))
- state_out_gradient: float32 [768, 64], P(('seq', 'batch'))
- state_skip_gradient: float32 [768], P(('seq', 'batch'))
- mixer_output_gradient: float32 [768, 768], P(('seq', 'batch'))
- first_gain_gradient: float32 [768], P(('seq', 'batch'))
- first_up_gradient: float32 [768, 3072], P(('seq', 'batch'))
- first_down_gradient: float32 [3072, 768], P(('seq', 'batch'))
- attend_gain_gradient: float32 [768], P(('seq', 'batch'))
- attend_inputs_gradient: float32 [768, 2304], P(('seq', 'batch'))
- attend_output_gradient: float32 [768, 768], P(('seq', 'batch'))
- second_gain_gradient: float32 [768], P(('seq', 'batch'))
- second_up_gradient: float32 [768, 3072], P(('seq', 'batch'))
- second_down_gradient: float32 [3072, 768], P(('seq', 'batch'))
Inputs may be any that keep to these rules, and one draw needn't show every extreme that they name: `lengths`: both ends are reached in every draw.
All inputs are finite; a program needn't handle non-finite values.
Results may differ from a plain program's by a relative error of at most 0.03.
Values may be sent and summed in bfloat16 or wider, within the bound.
A program may use at most 640 MiB of HBM per device.

v0:
```python
import jax
import jax.numpy as jnp
from jax import lax
from jax.sharding import PartitionSpec as P

HEADS = 12
HEAD_DIM = 64


eps = 1e-05
highest = lax.Precision.HIGHEST
masked_score = -1e30
group_width = 128


def passed_along(block, axis, distance):
    devices = range(lax.axis_size(axis))
    route = [(i - distance, i) for i in devices if i - distance in devices]
    return lax.ppermute(block, axis, route)


def entering(array, axis, join, neutral):
    place = lax.axis_index(axis)
    gathered = jax.tree.map(
        lambda a, kind: lax.all_gather(a.astype(kind), axis), array, (jnp.bfloat16, jnp.bfloat16)
    )
    state = jax.tree.map(lambda a, e: jnp.zeros_like(a) + jnp.asarray(e, a.dtype), array, neutral)

    def entering_one(hop, state):
        return join(
            state,
            jax.tree.map(
                lambda a, own: lax.dynamic_index_in_dim(a, hop, 0, False).astype(own.dtype),
                gathered,
                array,
            ),
        )

    return lax.fori_loop(0, place, entering_one, state)


def prefix(array, axis, join, neutral):
    count = lax.axis_size(axis)
    place = lax.axis_index(axis)
    ahead = count - 1 - place
    gathered = jax.tree.map(
        lambda a, kind: lax.all_gather(a.astype(kind), axis),
        array,
        jax.tree.map(lambda a: jnp.bfloat16 if a.dtype == jnp.float32 else a.dtype, array),
    )
    state = jax.tree.map(lambda a, e: jnp.zeros_like(a) + jnp.asarray(e, a.dtype), array, neutral)

    def prefix_one(hop, state):
        source = count - 1 - hop
        return join(
            state,
            jax.tree.map(
                lambda a, own: lax.dynamic_index_in_dim(a, source, 0, False).astype(own.dtype),
                gathered,
                array,
            ),
        )

    return lax.fori_loop(0, ahead, prefix_one, state)


def layer_norm(value, gain):
    centred = value - jnp.mean(value, axis=-1, keepdims=True)
    spread = jnp.mean(centred * centred, axis=-1, keepdims=True)
    return centred * lax.rsqrt(spread + eps) * gain


def gelu_tanh(value):
    return jax.nn.gelu(value, approximate=True)


def dense(left, weight):
    return jnp.dot(left, weight, preferred_element_type=jnp.float32)


def dense_back(left, weight, upstream):
    into_left = lax.dot_general(
        upstream, weight, (((1,), (1,)), ((), ())), preferred_element_type=jnp.float32
    )
    into_weight = lax.dot_general(
        left, upstream, (((0,), (0,)), ((), ())), preferred_element_type=jnp.float32
    )
    return (into_left, into_weight)


def split_groups(channels_last):
    seq_count, step_count, model_width = channels_last.shape
    grouped = channels_last.reshape(seq_count, step_count, model_width // group_width, group_width)
    return jnp.moveaxis(grouped, 2, 0)


def split_params(table):
    return table.reshape(table.shape[0] // group_width, group_width, table.shape[1])


def split_states(states):
    seq_count, model_width, state_count = states.shape
    return jnp.moveaxis(
        states.reshape(seq_count, model_width // group_width, group_width, state_count), 1, 0
    )


def join_states(grouped):
    group_count, seq_count, width_group, state_count = grouped.shape
    return jnp.moveaxis(grouped, 0, 1).reshape(seq_count, group_count * width_group, state_count)


def state_end(inner, decay_rate, state_in):
    step_count = inner.shape[1]
    remaining = (step_count - 1 - jnp.arange(step_count, dtype=jnp.int32)).astype(jnp.float32)

    def one_group(operand):
        inner_group, decay_group, input_group = operand
        weights = jnp.exp(-decay_group[None] * remaining[:, None, None]) * input_group[None]
        return jnp.einsum("stw,twn->swn", inner_group, weights, precision=highest)

    ends = lax.map(
        one_group, (split_groups(inner), split_params(decay_rate), split_params(state_in))
    )
    return join_states(ends)


def state_carry(inner, carried, decay_rate, state_in):
    return jnp.exp(-decay_rate * inner.shape[1]) * carried + state_end(inner, decay_rate, state_in)


def state_output(inner, carried, decay_rate, state_in, state_out, state_skip):
    seq_count, step_count, model_width = inner.shape
    steps = jnp.arange(step_count, dtype=jnp.int32)
    lag_matrix = steps[:, None] - steps[None, :]
    lag_index = jnp.maximum(lag_matrix, 0)
    causal_mask = (lag_matrix >= 0)[:, :, None]
    step_float = steps.astype(jnp.float32)

    def one_group(operand):
        inner_group, carried_group, decay_group, input_group, output_group = operand
        powers = jnp.exp(-decay_group[None] * step_float[:, None, None])
        kernel = jnp.einsum("wn,twn->tw", input_group * output_group, powers, precision=highest)
        toeplitz = jnp.where(causal_mask, kernel[lag_index], 0.0)
        local_part = jnp.einsum("trw,srw->stw", toeplitz, inner_group, precision=highest)
        reach = powers * jnp.exp(-decay_group)[None] * output_group[None]
        carry_part = jnp.einsum("twn,swn->stw", reach, carried_group, precision=highest)
        return local_part + carry_part

    mixed_groups = lax.map(
        one_group,
        (
            split_groups(inner),
            split_states(carried),
            split_params(decay_rate),
            split_params(state_in),
            split_params(state_out),
        ),
    )
    return (
        jnp.moveaxis(mixed_groups, 0, 2).reshape(seq_count, step_count, model_width)
        + state_skip * inner
    )


def chain(earlier, later):
    return (earlier[0] * later[0], later[0] * earlier[1] + later[1])


def shift_mix(extended, taps, value_part):
    step_count = value_part.shape[1]
    reach = taps.shape[1]
    shifted = extended[:, reach - 1 : reach - 1 + step_count] * taps[:, 0]
    for tap_index in range(1, reach):
        shifted = (
            shifted
            + extended[:, reach - 1 - tap_index : reach - 1 - tap_index + step_count]
            * taps[:, tap_index]
        )
    return shifted * value_part


def feed_forward(resid, gain, up_weight, down_weight):
    normed, norm_back = jax.vjp(layer_norm, resid, gain)
    normed_low = normed.astype(jnp.bfloat16)
    hidden = dense(normed_low, up_weight)
    active, active_back = jax.vjp(gelu_tanh, hidden)
    active_low = active.astype(jnp.bfloat16)
    return (
        resid + dense(active_low, down_weight),
        (norm_back, normed_low, active_back, active_low),
    )


def feed_back(stored, up_weight, down_weight, upstream):
    norm_back, normed_low, active_back, active_low = stored
    into_active, down_grad = dense_back(active_low, down_weight, upstream.astype(jnp.bfloat16))
    (into_hidden,) = active_back(into_active)
    into_normed, up_grad = dense_back(normed_low, up_weight, into_hidden.astype(jnp.bfloat16))
    into_resid, gain_grad = norm_back(into_normed)
    return (upstream + into_resid, gain_grad, up_grad, down_grad)


def split_blocks(array, block_len):
    shaped = array.reshape(
        (array.shape[0], array.shape[1] // block_len, block_len) + array.shape[2:]
    )
    return jnp.moveaxis(shaped, 1, 0)


def body(
    tokens,
    cotangent,
    lengths,
    mixer_gain,
    mixer_inputs,
    shift_taps,
    decay_rate,
    state_in,
    state_out,
    state_skip,
    mixer_output,
    first_gain,
    first_up,
    first_down,
    attend_gain,
    attend_inputs,
    attend_output,
    second_gain,
    second_up,
    second_down,
):
    shards = (
        mixer_gain,
        mixer_inputs,
        shift_taps,
        decay_rate,
        state_in,
        state_out,
        state_skip,
        mixer_output,
        first_gain,
        first_up,
        first_down,
        attend_gain,
        attend_inputs,
        attend_output,
        second_gain,
        second_up,
        second_down,
    )
    whole = (
        lax.all_gather(shards[0], ("seq", "batch"), axis=0, tiled=True),
        lax.all_gather(shards[1], ("seq", "batch"), axis=0, tiled=True),
        lax.all_gather(shards[2], ("seq", "batch"), axis=0, tiled=True),
        lax.all_gather(shards[3], ("seq", "batch"), axis=0, tiled=True),
        lax.all_gather(shards[4], ("seq", "batch"), axis=0, tiled=True),
        lax.all_gather(shards[5], ("seq", "batch"), axis=0, tiled=True),
        lax.all_gather(shards[6], ("seq", "batch"), axis=0, tiled=True),
        lax.all_gather(shards[7], ("seq", "batch"), axis=0, tiled=True),
        lax.all_gather(shards[8], ("seq", "batch"), axis=0, tiled=True),
        lax.all_gather(shards[9], ("seq", "batch"), axis=0, tiled=True),
        lax.all_gather(shards[10], ("seq", "batch"), axis=0, tiled=True),
        lax.all_gather(shards[11], ("seq", "batch"), axis=0, tiled=True),
        lax.all_gather(shards[12], ("seq", "batch"), axis=0, tiled=True),
        lax.all_gather(shards[13], ("seq", "batch"), axis=0, tiled=True),
        lax.all_gather(shards[14], ("seq", "batch"), axis=0, tiled=True),
        lax.all_gather(shards[15], ("seq", "batch"), axis=0, tiled=True),
        lax.all_gather(shards[16], ("seq", "batch"), axis=0, tiled=True),
    )
    seq_count, block_len, model_width = tokens.shape
    row_count = seq_count * block_len
    scale = HEAD_DIM ** (-0.5)
    rank_seq = lax.axis_index("seq")
    offsets = jnp.arange(block_len, dtype=jnp.int32)
    places = rank_seq * block_len + offsets
    valid = (places[None, :] < lengths[:, None]).astype(jnp.float32)
    longest = jnp.max(lengths)
    any_live = places[0] < longest
    gain_mixer = whole[0].astype(jnp.float32)
    taps_float = whole[2].astype(jnp.float32)
    decay_float = whole[3].astype(jnp.float32)
    input_float = whole[4].astype(jnp.float32)
    output_float = whole[5].astype(jnp.float32)
    skip_float = whole[6].astype(jnp.float32)
    gain_first = whole[8].astype(jnp.float32)
    gain_attend = whole[11].astype(jnp.float32)
    gain_second = whole[14].astype(jnp.float32)
    start_resid = tokens.reshape(row_count, model_width).astype(jnp.float32)
    normed_mixer, back_mixer = jax.vjp(layer_norm, start_resid, gain_mixer)
    normed_low_mixer = normed_mixer.astype(jnp.bfloat16)
    projected = dense(normed_low_mixer, whole[1])
    query_mixer = projected[:, :model_width]
    keys_mixer = projected[:, model_width : 2 * model_width].reshape(
        seq_count, block_len, model_width
    )
    value_mixer = projected[:, 2 * model_width :].reshape(seq_count, block_len, model_width)
    reach = taps_float.shape[1]
    rim_rows = passed_along(keys_mixer[:, block_len - reach + 1 :], "seq", 1)
    extended = jnp.concatenate([rim_rows, keys_mixer], axis=1)
    inner, shift_back = jax.vjp(shift_mix, extended, taps_float, value_mixer)
    ends = state_end(inner, decay_float, input_float)
    power = jnp.exp(-decay_float * block_len)
    scanned = entering((power, ends), "seq", chain, (jnp.ones_like(power), jnp.zeros_like(ends)))
    carried = scanned[1]
    state_y, output_back = jax.vjp(
        state_output, inner, carried, decay_float, input_float, output_float, skip_float
    )
    state_flat = state_y.reshape(row_count, model_width)
    gated_low = (query_mixer * state_flat).astype(jnp.bfloat16)
    resid_mixer = start_resid + dense(gated_low, whole[7])
    resid_first, stored_first = feed_forward(resid_mixer, gain_first, whole[9], whole[10])
    normed_attend, back_attend = jax.vjp(layer_norm, resid_first, gain_attend)
    normed_low_attend = normed_attend.astype(jnp.bfloat16)
    proj_low = dense(normed_low_attend, whole[12]).astype(jnp.bfloat16)
    head_shape = (seq_count, block_len, HEADS, HEAD_DIM)
    query_low = proj_low[:, :model_width].reshape(head_shape)
    keys_low = proj_low[:, model_width : 2 * model_width].reshape(head_shape)
    value_low = proj_low[:, 2 * model_width :].reshape(head_shape)

    def block_scores(queries, keys_block, query_places, key_places):
        scores = (
            jnp.einsum("sqhe,skhe->sqhk", queries, keys_block, preferred_element_type=jnp.float32)
            * scale
        )
        causal_mask = key_places[None, :] <= query_places[:, None]
        return jnp.where(causal_mask[None, :, None, :], scores, masked_score)

    def key_needed(key_first):
        return (key_first <= places[-1]) & ((key_first == places[0]) | any_live)

    stat_shape = (seq_count, block_len, HEADS)
    start_state = (
        jnp.full(stat_shape, masked_score, jnp.float32),
        jnp.zeros(stat_shape, jnp.float32),
        jnp.zeros(head_shape, jnp.float32),
    )
    shard_piece = (
        lax.all_gather(keys_low, "seq", axis=1, tiled=True),
        lax.all_gather(value_low, "seq", axis=1, tiled=True),
    )
    keys_blocks = split_blocks(shard_piece[0], block_len)
    value_blocks = split_blocks(shard_piece[1], block_len)
    firsts = jnp.arange(keys_blocks.shape[0], dtype=jnp.int32) * block_len

    def attend_one_step(state_now, operand):
        keys_block, value_block, key_first = operand

        def attend_work(state_in_block):
            running_max, running_sum, running_out = state_in_block
            scores = block_scores(query_low, keys_block, places, key_first + offsets)
            new_max = jnp.maximum(running_max, jnp.max(scores, axis=-1))
            fade = jnp.exp(running_max - new_max)
            shifted = jnp.exp(scores - new_max[..., None])
            new_sum = running_sum * fade + jnp.sum(shifted, axis=-1)
            new_out = running_out * fade[..., None] + jnp.einsum(
                "sqhk,skhe->sqhe",
                shifted.astype(jnp.bfloat16),
                value_block,
                preferred_element_type=jnp.float32,
            )
            return (new_max, new_sum, new_out)

        return (
            lax.cond(
                key_needed(key_first), attend_work, lambda state_in_block: state_in_block, state_now
            ),
            None,
        )

    result, _ = lax.scan(attend_one_step, start_state, (keys_blocks, value_blocks, firsts))
    running_max, running_sum, running_out = result
    attended = running_out / running_sum[..., None]
    logsum = running_max + jnp.log(running_sum)
    attended_low = attended.reshape(row_count, model_width).astype(jnp.bfloat16)
    resid_attend = resid_first + dense(attended_low, whole[13])
    final, stored_second = feed_forward(resid_attend, gain_second, whole[15], whole[16])
    mixed = (final.reshape(seq_count, block_len, model_width) * valid[..., None]).astype(
        jnp.bfloat16
    )
    whole = (
        lax.all_gather(shards[0], ("seq", "batch"), axis=0, tiled=True),
        lax.all_gather(shards[1], ("seq", "batch"), axis=0, tiled=True),
        lax.all_gather(shards[2], ("seq", "batch"), axis=0, tiled=True),
        lax.all_gather(shards[3], ("seq", "batch"), axis=0, tiled=True),
        lax.all_gather(shards[4], ("seq", "batch"), axis=0, tiled=True),
        lax.all_gather(shards[5], ("seq", "batch"), axis=0, tiled=True),
        lax.all_gather(shards[6], ("seq", "batch"), axis=0, tiled=True),
        lax.all_gather(shards[7], ("seq", "batch"), axis=0, tiled=True),
        lax.all_gather(shards[8], ("seq", "batch"), axis=0, tiled=True),
        lax.all_gather(shards[9], ("seq", "batch"), axis=0, tiled=True),
        lax.all_gather(shards[10], ("seq", "batch"), axis=0, tiled=True),
        lax.all_gather(shards[11], ("seq", "batch"), axis=0, tiled=True),
        lax.all_gather(shards[12], ("seq", "batch"), axis=0, tiled=True),
        lax.all_gather(shards[13], ("seq", "batch"), axis=0, tiled=True),
        lax.all_gather(shards[14], ("seq", "batch"), axis=0, tiled=True),
        lax.all_gather(shards[15], ("seq", "batch"), axis=0, tiled=True),
        lax.all_gather(shards[16], ("seq", "batch"), axis=0, tiled=True),
    )
    upstream = (cotangent.astype(jnp.float32) * valid[..., None]).reshape(row_count, model_width)
    upstream, second_gain_grad, second_up_grad, second_down_grad = feed_back(
        stored_second, whole[15], whole[16], upstream
    )
    into_attended, attend_output_grad = dense_back(
        attended_low, whole[13], upstream.astype(jnp.bfloat16)
    )
    dout_low = into_attended.astype(jnp.bfloat16).reshape(head_shape)
    delta = jnp.sum(dout_low.astype(jnp.float32) * attended, axis=-1)
    shard_piece = (
        lax.all_gather(keys_low, "seq", axis=1, tiled=True),
        lax.all_gather(value_low, "seq", axis=1, tiled=True),
    )
    keys_blocks = split_blocks(shard_piece[0], block_len)
    value_blocks = split_blocks(shard_piece[1], block_len)
    firsts = jnp.arange(keys_blocks.shape[0], dtype=jnp.int32) * block_len

    def query_one_step(query_grad, operand):
        keys_block, value_block, key_first = operand

        def query_work(grad_now):
            scores = block_scores(query_low, keys_block, places, key_first + offsets)
            soft = jnp.exp(scores - logsum[..., None])
            dprob = jnp.einsum(
                "sqhe,skhe->sqhk", dout_low, value_block, preferred_element_type=jnp.float32
            )
            dscore = (soft * (dprob - delta[..., None])).astype(jnp.bfloat16)
            return (
                grad_now
                + jnp.einsum(
                    "sqhk,skhe->sqhe", dscore, keys_block, preferred_element_type=jnp.float32
                )
                * scale
            )

        return (
            lax.cond(key_needed(key_first), query_work, lambda grad_now: grad_now, query_grad),
            None,
        )

    result, _ = lax.scan(
        query_one_step, jnp.zeros(head_shape, jnp.float32), (keys_blocks, value_blocks, firsts)
    )
    query_grad = result
    sent = (query_low.astype(jnp.float32), dout_low.astype(jnp.float32), logsum, delta)
    shard_piece = (
        lax.all_gather(sent[0].astype(jnp.bfloat16), "seq", axis=1, tiled=True).astype(jnp.float32),
        lax.all_gather(sent[1].astype(jnp.bfloat16), "seq", axis=1, tiled=True).astype(jnp.float32),
        lax.all_gather(sent[2].astype(jnp.bfloat16), "seq", axis=1, tiled=True).astype(jnp.float32),
        lax.all_gather(sent[3].astype(jnp.bfloat16), "seq", axis=1, tiled=True).astype(jnp.float32),
    )
    query_blocks = split_blocks(shard_piece[0], block_len)
    dout_blocks = split_blocks(shard_piece[1], block_len)
    logsum_blocks = split_blocks(shard_piece[2], block_len)
    delta_blocks = split_blocks(shard_piece[3], block_len)
    firsts = jnp.arange(query_blocks.shape[0], dtype=jnp.int32) * block_len

    def key_one_step(grads_now, operand):
        query_block, dout_block, logsum_block, delta_block, query_first = operand

        def key_work(grads_in):
            keys_grad, value_grad = grads_in
            query_cast = query_block.astype(jnp.bfloat16)
            dout_cast = dout_block.astype(jnp.bfloat16)
            scores = block_scores(query_cast, keys_low, query_first + offsets, places)
            soft = jnp.exp(scores - logsum_block[..., None])
            value_grad = value_grad + jnp.einsum(
                "sqhk,sqhe->skhe",
                soft.astype(jnp.bfloat16),
                dout_cast,
                preferred_element_type=jnp.float32,
            )
            dprob = jnp.einsum(
                "sqhe,skhe->sqhk", dout_cast, value_low, preferred_element_type=jnp.float32
            )
            dscore = (soft * (dprob - delta_block[..., None])).astype(jnp.bfloat16)
            keys_grad = (
                keys_grad
                + jnp.einsum(
                    "sqhk,sqhe->skhe", dscore, query_cast, preferred_element_type=jnp.float32
                )
                * scale
            )
            return (keys_grad, value_grad)

        needed = (query_first + block_len - 1 >= places[0]) & (
            (query_first == places[0]) | (query_first < longest)
        )
        return (lax.cond(needed, key_work, lambda grads_in: grads_in, grads_now), None)

    result, _ = lax.scan(
        key_one_step,
        (jnp.zeros(head_shape, jnp.float32), jnp.zeros(head_shape, jnp.float32)),
        (query_blocks, dout_blocks, logsum_blocks, delta_blocks, firsts),
    )
    keys_grad, value_grad = result
    proj_grad = jnp.concatenate(
        [
            query_grad.reshape(row_count, model_width),
            keys_grad.reshape(row_count, model_width),
            value_grad.reshape(row_count, model_width),
        ],
        axis=1,
    ).astype(jnp.bfloat16)
    into_normed, attend_inputs_grad = dense_back(normed_low_attend, whole[12], proj_grad)
    into_resid, attend_gain_grad = back_attend(into_normed)
    later_block = (
        attend_gain_grad,
        attend_inputs_grad,
        attend_output_grad,
        second_gain_grad,
        second_up_grad,
        second_down_grad,
    )
    upstream = upstream + into_resid
    upstream, first_gain_grad, first_up_grad, first_down_grad = feed_back(
        stored_first, whole[9], whole[10], upstream
    )
    into_gated, mixer_output_grad = dense_back(gated_low, whole[7], upstream.astype(jnp.bfloat16))
    query_mixer_grad = into_gated * state_flat
    state_grad = (into_gated * query_mixer).reshape(seq_count, block_len, model_width)
    inner_grad_a, carried_grad, decay_grad_a, input_grad_a, output_grad, skip_grad = output_back(
        state_grad
    )
    scanned_back = prefix(
        (power, carried_grad), "seq", chain, (jnp.ones_like(power), jnp.zeros_like(carried_grad))
    )
    later_grad = scanned_back[1]
    _, carry_back = jax.vjp(state_carry, inner, carried, decay_float, input_float)
    inner_grad_b, _, decay_grad_b, input_grad_b = carry_back(later_grad)
    extended_grad, taps_grad, value_mixer_grad = shift_back(inner_grad_a + inner_grad_b)
    spill = passed_along(extended_grad[:, : reach - 1], "seq", -1)
    keys_mixer_grad = extended_grad[:, reach - 1 :] + jnp.pad(
        spill, ((0, 0), (block_len - reach + 1, 0), (0, 0))
    )
    proj_grad_mixer = jnp.concatenate(
        [
            query_mixer_grad,
            keys_mixer_grad.reshape(row_count, model_width),
            value_mixer_grad.reshape(row_count, model_width),
        ],
        axis=1,
    ).astype(jnp.bfloat16)
    into_normed_mixer, mixer_inputs_grad = dense_back(normed_low_mixer, whole[1], proj_grad_mixer)
    into_start, mixer_gain_grad = back_mixer(into_normed_mixer)
    tokens_gradient = (
        (upstream + into_start).reshape(seq_count, block_len, model_width).astype(jnp.bfloat16)
    )
    earlier_block = (
        mixer_gain_grad,
        mixer_inputs_grad,
        taps_grad,
        decay_grad_a + decay_grad_b,
        input_grad_a + input_grad_b,
        output_grad,
        skip_grad,
        mixer_output_grad,
        first_gain_grad,
        first_up_grad,
        first_down_grad,
    )
    grads = earlier_block + later_block
    summed = tuple(lax.psum_scatter(grads, ("seq", "batch"), scatter_dimension=0, tiled=True))
    return (mixed, tokens_gradient) + tuple(summed)


def solution(mesh):
    return jax.shard_map(
        body,
        mesh=mesh,
        in_specs=(
            P("batch", "seq", None),
            P("batch", "seq", None),
            P("batch"),
            P(("seq", "batch")),
            P(("seq", "batch"), None),
            P(("seq", "batch"), None),
            P(("seq", "batch"), None),
            P(("seq", "batch"), None),
            P(("seq", "batch"), None),
            P(("seq", "batch")),
            P(("seq", "batch"), None),
            P(("seq", "batch")),
            P(("seq", "batch"), None),
            P(("seq", "batch"), None),
            P(("seq", "batch")),
            P(("seq", "batch"), None),
            P(("seq", "batch"), None),
            P(("seq", "batch")),
            P(("seq", "batch"), None),
            P(("seq", "batch"), None),
        ),
        out_specs=(
            P("batch", "seq", None),
            P("batch", "seq", None),
            P(("seq", "batch")),
            P(("seq", "batch"), None),
            P(("seq", "batch"), None),
            P(("seq", "batch"), None),
            P(("seq", "batch"), None),
            P(("seq", "batch"), None),
            P(("seq", "batch")),
            P(("seq", "batch"), None),
            P(("seq", "batch")),
            P(("seq", "batch"), None),
            P(("seq", "batch"), None),
            P(("seq", "batch")),
            P(("seq", "batch"), None),
            P(("seq", "batch"), None),
            P(("seq", "batch")),
            P(("seq", "batch"), None),
            P(("seq", "batch"), None),
        ),
        check_vma=False,
    )
```

profile of v0, /device:TPU:0, one launch (start us, length us, event | category | flops | bytes accessed | tf_op | source)
XLA Modules:
  0.0 4405.6 jit_solution(7096263292405181731)
XLA Ops:
  367.3 887.2 %while.178 = (s32[]{:T(128)}, f32[6,2,128,128]{2,1,3,0:T(2,128)S(1)}, f32[6,128,128,64]{1,3,2,0:T(8,128)}, f32[6,128,64]{2,1,0:T(8,128)}, f32[6,128,128,128]{2,1...) while((s32[]{:T(128)}, ...), condition=%wide.region_7.8_spmd.clone.clone, body=%wide.region_6.7_spmd.clone.clone.sunk | while | flops 99729536 | bytes 157424304 | solution.py:150
  1285.7 83.5 %all-gather.31.cloned.1.call-done = bf16[2,1024,12,64]{1,0,3,2:T(2,128)(2,1)} async-done(((bf16[2,128,12,64]{1,0,3,2:T(2,128)(2,1)}), bf16[2,1024,12,64]{1,0,3,2:T(2,128)(2,1)}) %all-gather.31.cloned.1.call-update) | async-done | bytes 3145744 | tf_op jit(solution)/shard_map/all_gather | solution.py:340
  1379.6 76.9 %all-gather.29.cloned.1.call-done = bf16[2,1024,12,64]{1,0,3,2:T(2,128)(2,1)} async-done(((bf16[2,128,12,64]{1,0,3,2:T(2,128)(2,1)}), bf16[2,1024,12,64]{1,0,3,2:T(2,128)(2,1)}) %all-gather.29.cloned.1.call-update) | async-done | bytes 3145744 | tf_op jit(solution)/shard_map/all_gather | solution.py:339
  1517.9 60.7 %all-gather.35.cloned.1.call-done = bf16[768,3072]{1,0:T(8,128)(2,1)} async-done(((bf16[24,3072]{1,0:T(8,128)(2,1)}), bf16[768,3072]{1,0:T(8,128)(2,1)}) %all-gather.35.cloned.1.call-update) | async-done | bytes 4718608 | tf_op jit(solution)/shard_map/all_gather | solution.py:268
  1584.2 59.2 %all-gather.37.cloned.1.call-done = bf16[3072,768]{1,0:T(8,128)(2,1)} async-done(((bf16[96,768]{1,0:T(8,128)(2,1)}), bf16[3072,768]{1,0:T(8,128)(2,1)}) %all-gather.37.cloned.1.call-update) | async-done | bytes 4718608 | tf_op jit(solution)/shard_map/all_gather | solution.py:269
  1775.8 57.5 %while.174 = (s32[]{:T(128)}, f32[2,128,12,64]{1,3,2,0:T(8,128)S(1)}, f32[2,128,12,64]{1,3,2,0:T(8,128)S(1)}, s32[8]{0:T(128)}, s32[128]{0:T(128)}, /*index=5*/s...) while((s32[]{:T(128)}, ...), condition=%wide.region_31.32_spmd.clone, body=%wide.region_28.31_spmd.clone.sunk | while | flops 204685440 | bytes 10339155 | solution.py:490
  1857.1 1023.8 %while.175 = (s32[]{:T(128)}, f32[6,2,128,128]{2,1,3,0:T(2,128)}, bf16[6,2,128,64]{3,1,2,0:T(2,128)(2,1)}, f32[6,128,64]{2,1,0:T(8,128)}, f32[6,128,64]{2,1,0:T(...) while((s32[]{:T(128)}, f32[6,2,128,128]{2,1,3,0:T(2,128)}, ...), condition=%wide.region_41.42_spmd.clone, body=%wide.region_36.41_spmd.clone.sunk | while | flops 179372160 | bytes 52944108 | solution.py:150
  1882.9 98.3 %scatter_custom_fusion.6 = f32[128,128]{1,0:T(8,128)S(1)} fusion(s32[16384]{0:T(1024)S(1)} %maximum_bitcast_fusion.2, f32[16384,128]{1,0:T(8,128)} %bitcast.695, f32[]{:T(128)} %constant.376.clone.1..sunk), kind=kCustom, calls=%fused_computation.153.clone.1 | custom fusion | flops 2097152 | bytes 66048 | tf_op jit(solution)/shard_map/transpose(jvp())/while/body/eval_jaxpr/scatter-add | solution.py:144
  2053.4 98.3 %scatter_custom_fusion.6 = f32[128,128]{1,0:T(8,128)S(1)} fusion(s32[16384]{0:T(1024)S(1)} %maximum_bitcast_fusion.2, f32[16384,128]{1,0:T(8,128)} %bitcast.695, f32[]{:T(128)} %constant.376.clone.1..sunk), kind=kCustom, calls=%fused_computation.153.clone.1 | custom fusion | flops 2097152 | bytes 66048 | tf_op jit(solution)/shard_map/transpose(jvp())/while/body/eval_jaxpr/scatter-add | solution.py:144
  2224.0 98.3 %scatter_custom_fusion.6 = f32[128,128]{1,0:T(8,128)S(1)} fusion(s32[16384]{0:T(1024)S(1)} %maximum_bitcast_fusion.2, f32[16384,128]{1,0:T(8,128)} %bitcast.695, f32[]{:T(128)} %constant.376.clone.1..sunk), kind=kCustom, calls=%fused_computation.153.clone.1 | custom fusion | flops 2097152 | bytes 66048 | tf_op jit(solution)/shard_map/transpose(jvp())/while/body/eval_jaxpr/scatter-add | solution.py:144
  2394.5 98.3 %scatter_custom_fusion.6 = f32[128,128]{1,0:T(8,128)S(1)} fusion(s32[16384]{0:T(1024)S(1)} %maximum_bitcast_fusion.2, f32[16384,128]{1,0:T(8,128)} %bitcast.695, f32[]{:T(128)} %constant.376.clone.1..sunk), kind=kCustom, calls=%fused_computation.153.clone.1 | custom fusion | flops 2097152 | bytes 66048 | tf_op jit(solution)/shard_map/transpose(jvp())/while/body/eval_jaxpr/scatter-add | solution.py:144
  2565.1 98.3 %scatter_custom_fusion.6 = f32[128,128]{1,0:T(8,128)S(1)} fusion(s32[16384]{0:T(1024)S(1)} %maximum_bitcast_fusion.2, f32[16384,128]{1,0:T(8,128)} %bitcast.695, f32[]{:T(128)} %constant.376.clone.1..sunk), kind=kCustom, calls=%fused_computation.153.clone.1 | custom fusion | flops 2097152 | bytes 66048 | tf_op jit(solution)/shard_map/transpose(jvp())/while/body/eval_jaxpr/scatter-add | solution.py:144
  2735.6 98.3 %scatter_custom_fusion.6 = f32[128,128]{1,0:T(8,128)S(1)} fusion(s32[16384]{0:T(1024)S(1)} %maximum_bitcast_fusion.2, f32[16384,128]{1,0:T(8,128)} %bitcast.695, f32[]{:T(128)} %constant.376.clone.1..sunk), kind=kCustom, calls=%fused_computation.153.clone.1 | custom fusion | flops 2097152 | bytes 66048 | tf_op jit(solution)/shard_map/transpose(jvp())/while/body/eval_jaxpr/scatter-add | solution.py:144
  2908.1 201.4 %while.176 = (s32[]{:T(128)}, f32[6,128,128,64]{1,3,2,0:T(8,128)}, f32[6,1,128,64]{3,2,1,0:T(8,128)S(1)}, f32[6,128,128,64]{1,3,2,0:T(8,128)}, f32[6,128,64]{2,1...) while((s32[]{:T(128)}, f32[6,128,128,64]{1,3,2,0:T(8,128)}, ...), condition=%wide.region_45.46_spmd.clone, body=%wide.region_44.45_spmd.clone.sunk | while | flops 2105602 | bytes 42272852 | solution.py:122
  3129.6 106.7 %while.177 = (s32[]{:T(128)}, f32[6,2,128,128]{2,1,3,0:T(2,128)S(1)}, f32[6,128,64]{2,1,0:T(8,128)}, f32[6,128,64]{2,1,0:T(8,128)}, f32[6,2,128,64]{3,1,2,0:T(2,...) while((s32[]{:T(128)}, ...), condition=%wide.region_49.50_spmd.clone, body=%wide.region_46.49_spmd.clone.sunk | while | flops 56615168 | bytes 9310337 | solution.py:122
  3313.9 82.0 %all-reduce.23 = (f32[768]{0:T(1024)S(1)}, f32[768,4]{0,1:T(4,128)S(1)}, f32[768]{0:T(1024)S(1)}, f32[768]{0:T(1024)S(1)}, f32[768]{0:T(1024)S(1)}, /*index=5*/f32[768]{0:T(1024)S(1)}) all-reduce(f32[768]{0:T(1024)S(1)} %get-tuple-element.2309, ...), channel_id=3, replica_groups=mesh['seq'=8,'batch'=4] {'seq','batch'}, use_global_device_ids=true, to_apply=%region_53.54.clone | all-reduce | flops 6912 | bytes 55296
  3400.5 78.2 %reduce-scatter.35.cloned.1.call-done = f32[24,64]{1,0:T(8,128)} async-done(((f32[768,64]{1,0:T(8,128)}), f32[24,64]{1,0:T(8,128)}) %reduce-scatter.35.cloned.1.call-update) | async-done | bytes 6160
  3478.7 104.5 %reduce-scatter.21.cloned.1.call-done = f32[24,768]{1,0:T(8,128)} async-done(((f32[768,768]{1,0:T(8,128)}), f32[24,768]{1,0:T(8,128)}) %reduce-scatter.21.cloned.1.call-update) | async-done | bytes 73744 | tf_op jit(solution)/shard_map/reduce_scatter | solution.py:562
  3583.2 141.5 %reduce-scatter.33.cloned.1.call-done = f32[96,768]{1,0:T(8,128)} async-done(((f32[3072,768]{1,0:T(8,128)}), f32[96,768]{1,0:T(8,128)}) %reduce-scatter.33.cloned.1.call-update) | async-done | bytes 294928 | tf_op jit(solution)/shard_map/reduce_scatter | solution.py:562
  3724.7 141.6 %reduce-scatter.31.cloned.1.call-done = f32[24,3072]{1,0:T(8,128)} async-done(((f32[768,3072]{1,0:T(8,128)}), f32[24,3072]{1,0:T(8,128)}) %reduce-scatter.31.cloned.1.call-update) | async-done | bytes 294928 | tf_op jit(solution)/shard_map/reduce_scatter | solution.py:562
  3866.3 124.6 %reduce-scatter.27.cloned.1.call-done = f32[24,2304]{1,0:T(8,128)} async-done(((f32[768,2304]{1,0:T(8,128)}), f32[24,2304]{1,0:T(8,128)}) %reduce-scatter.27.cloned.1.call-update) | async-done | bytes 221200 | tf_op jit(solution)/shard_map/reduce_scatter | solution.py:562
  3991.0 124.8 %reduce-scatter.19.cloned.1.call-done = f32[24,2304]{1,0:T(8,128)} async-done(((f32[768,2304]{1,0:T(8,128)}), f32[24,2304]{1,0:T(8,128)}) %reduce-scatter.19.cloned.1.call-update) | async-done | bytes 221200 | tf_op jit(solution)/shard_map/reduce_scatter | solution.py:562
  4115.7 141.5 %reduce-scatter.25.cloned.1.call-done = f32[96,768]{1,0:T(8,128)} async-done(((f32[3072,768]{1,0:T(8,128)}), f32[96,768]{1,0:T(8,128)}) %reduce-scatter.25.cloned.1.call-update) | async-done | bytes 294928 | tf_op jit(solution)/shard_map/reduce_scatter | solution.py:562
  4257.3 141.6 %reduce-scatter.23.cloned.1.call-done = f32[24,3072]{1,0:T(8,128)} async-done(((f32[768,3072]{1,0:T(8,128)}), f32[24,3072]{1,0:T(8,128)}) %reduce-scatter.23.cloned.1.call-update) | async-done | bytes 294928 | tf_op jit(solution)/shard_map/reduce_scatter | solution.py:562
  (1017 shorter events, 2560.4 us)
Async XLA Ops:
  7.9 319.9 %all-gather.19.cloned.1.call-start = ((), (), s32[]{:S(2)}) async-start(), calls=%async_computation.12 | async-start | bytes 1769472 | tf_op jit(solution)/shard_map/all_gather | solution.py:25
  243.8 1015.4 %all-gather.21.cloned.1.call-start = ((), (), s32[]{:S(2)}) async-start(), calls=%async_computation.13 | async-start | bytes 1216512 | tf_op jit(solution)/shard_map/all_gather | solution.py:260
  244.6 1016.9 %all-gather.23.cloned.1.call-start = ((), (), s32[]{:S(2)}) async-start(), calls=%async_computation.14 | async-start | bytes 4866048 | tf_op jit(solution)/shard_map/all_gather | solution.py:262
  245.1 1021.9 %all-gather.25.cloned.1.call-start = ((), (), s32[]{:S(2)}) async-start(), calls=%async_computation.15 | async-start | bytes 4866048 | tf_op jit(solution)/shard_map/all_gather | solution.py:263
  245.7 1027.0 %all-gather.27.cloned.1.call-start = ((), (), s32[]{:S(2)}) async-start(), calls=%async_computation.16 | async-start | bytes 3649536 | tf_op jit(solution)/shard_map/all_gather | solution.py:265
  246.3 1122.9 %all-gather.31.cloned.1.call-start = ((), (), s32[]{:S(2)}) async-start(), calls=%async_computation.18 | async-start | bytes 3538944 | tf_op jit(solution)/shard_map/all_gather | solution.py:340
  1277.6 178.9 %all-gather.29.cloned.1.call-start = ((), (), s32[]{:S(2)}) async-start(), calls=%async_computation.17 | async-start | bytes 3538944 | tf_op jit(solution)/shard_map/all_gather | solution.py:339
  1278.7 236.9 %all-gather.33.cloned.1.call-start = ((), (), s32[]{:S(2)}) async-start(), calls=%async_computation.19 | async-start | bytes 1216512 | tf_op jit(solution)/shard_map/all_gather | solution.py:266
  1279.4 299.2 %all-gather.35.cloned.1.call-start = ((), (), s32[]{:S(2)}) async-start(), calls=%async_computation.20 | async-start | bytes 4866048 | tf_op jit(solution)/shard_map/all_gather | solution.py:268
  1280.0 363.4 %all-gather.37.cloned.1.call-start = ((), (), s32[]{:S(2)}) async-start(), calls=%async_computation.21 | async-start | bytes 4866048 | tf_op jit(solution)/shard_map/all_gather | solution.py:269
  1280.7 429.0 %all-gather.39.cloned.1.call-start = ((), (), s32[]{:S(2)}) async-start(), calls=%async_computation.22 | async-start | bytes 3538944 | tf_op jit(solution)/shard_map/all_gather | solution.py:446
  1285.6 484.8 %all-gather.41.cloned.1.call-start = ((), (), s32[]{:S(2)}) async-start(), calls=%async_computation.23 | async-start | bytes 3538944 | tf_op jit(solution)/shard_map/all_gather | solution.py:447
  1659.5 1450.0 %all-gather.43.cloned.1.call-start = ((), (), s32[]{:S(2)}) async-start(), calls=%async_computation.24 | async-start | bytes 1769472 | tf_op jit(solution)/shard_map/all_gather | solution.py:47
  2882.9 517.6 %reduce-scatter.29.cloned.1.call-start = ((), (), s32[]{:S(2)}) async-start(), calls=%async_computation.30 | async-start | bytes 2433024 | tf_op jit(solution)/shard_map/reduce_scatter | solution.py:562
  2884.9 515.6 %reduce-scatter.39.cloned.1.call-start = ((), (), s32[]{:S(2)}) async-start(), calls=%async_computation.35 | async-start | bytes 405504
  3109.5 291.0 %reduce-scatter.37.cloned.1.call-start = ((), (), s32[]{:S(2)}) async-start(), calls=%async_computation.34 | async-start | bytes 405504
  3239.4 239.2 %reduce-scatter.35.cloned.1.call-start = ((), (), s32[]{:S(2)}) async-start(), calls=%async_computation.33 | async-start | bytes 405504
  3241.6 341.5 %reduce-scatter.21.cloned.1.call-start = ((), (), s32[]{:S(2)}) async-start(), calls=%async_computation.26 | async-start | bytes 2433024 | tf_op jit(solution)/shard_map/reduce_scatter | solution.py:562
  3243.7 481.1 %reduce-scatter.33.cloned.1.call-start = ((), (), s32[]{:S(2)}) async-start(), calls=%async_computation.32 | async-start | bytes 9732096 | tf_op jit(solution)/shard_map/reduce_scatter | solution.py:562
  3251.6 614.7 %reduce-scatter.31.cloned.1.call-start = ((), (), s32[]{:S(2)}) async-start(), calls=%async_computation.31 | async-start | bytes 9732096 | tf_op jit(solution)/shard_map/reduce_scatter | solution.py:562
  3258.4 732.6 %reduce-scatter.27.cloned.1.call-start = ((), (), s32[]{:S(2)}) async-start(), calls=%async_computation.29 | async-start | bytes 7299072 | tf_op jit(solution)/shard_map/reduce_scatter | solution.py:562
  3264.0 851.7 %reduce-scatter.19.cloned.1.call-start = ((), (), s32[]{:S(2)}) async-start(), calls=%async_computation.25 | async-start | bytes 7299072 | tf_op jit(solution)/shard_map/reduce_scatter | solution.py:562
  3283.5 973.8 %reduce-scatter.25.cloned.1.call-start = ((), (), s32[]{:S(2)}) async-start(), calls=%async_computation.28 | async-start | bytes 9732096 | tf_op jit(solution)/shard_map/reduce_scatter | solution.py:562
  3292.4 1106.5 %reduce-scatter.23.cloned.1.call-start = ((), (), s32[]{:S(2)}) async-start(), calls=%async_computation.27 | async-start | bytes 9732096 | tf_op jit(solution)/shard_map/reduce_scatter | solution.py:562
  (156 other events, 5566.7 us)
Sparse Core Ops, SparseCore 0:
  10.9 63.0 all-gather.16
  298.7 53.0 all-gather.20
  354.5 62.4 all-gather.22
  419.8 61.8 all-gather.24
  484.4 58.3 all-gather.26
  1277.7 91.4 all-gather.30
  1371.2 85.1 all-gather.28
  1459.3 53.9 all-gather.32
  1516.1 62.4 all-gather.34
  1581.5 61.8 all-gather.36
  1645.3 61.8 all-gather.38
  1709.2 61.1 all-gather.40
  2883.0 87.2 all-gather.42
  2976.0 97.9 reduce-scatter.28
  3109.6 138.8 reduce-scatter.38
  3253.9 124.5 reduce-scatter.36
  3383.9 94.6 reduce-scatter.34
  3484.5 98.6 reduce-scatter.20
  3589.5 135.1 reduce-scatter.32
  3731.2 135.0 reduce-scatter.30
  3872.6 118.3 reduce-scatter.26
  3997.2 118.4 reduce-scatter.18
  4122.1 135.1 reduce-scatter.24
  4263.7 135.0 reduce-scatter.22
  (1 shorter events, 51.7 us)
where the time goes:
time: 4430 us; the launch traced here: 4410 us
  waiting for transfers between devices  1290 us (29%)
  local copies, waits for them, and re-layouts  1070 us (24%)
  other arithmetic  802 us (18%)
  matrix products  784 us (18%)
  blocking collectives  366 us (8%)
  loops' own time  74.6 us (2%)
    reduce_scatter x8, waiting for transfers between devices, body(): lax.psum_scatter(grads, ('seq', 'batch'), scatter_dimension=0, tiled=True)  920 us
    scatter-add x6, other arithmetic, one_group(): toeplitz = jnp.where(causal_mask, kernel[lag_index], 0.0)  590 us
    dynamic_update_slice x66, local copies, waits for them, and re-layouts, state_output(): lax.map(one_group, (split_groups(inner), split_states(carried), split_par...  386 us
    gather x12, local copies, waits for them, and re-layouts, one_group(): toeplitz = jnp.where(causal_mask, kernel[lag_index], 0.0)  383 us
    dot_general x18, matrix products, one_group(): jnp.einsum('trw,srw->stw', toeplitz, inner_group, precision=highest)  256 us
    dot_general x18, matrix products, one_group(): jnp.einsum('twn,swn->stw', reach, carried_group, precision=highest)  190 us
    dot_general x18, matrix products, one_group(): return jnp.einsum('stw,twn->swn', inner_group, weights, precision=highest)  159 us
    unnamed x2, blocking collectives  124 us
  transfers between devices with their start and end apart: 27, of which 14 were waited for; matrix products, arithmetic and copies ran while one was open for 34% of the time, Pallas kernels for 0%

commit v1 on v0

v1 whole, which is shorter than its diff:
```python
import functools

import jax
import jax.numpy as jnp
from jax import lax
from jax.experimental import pallas as pl
from jax.experimental.pallas import tpu as pltpu
from jax.sharding import PartitionSpec as P

HEADS = 12
HEAD_DIM = 64

eps = 1e-05
masked_score = -1e30
lanes = 128
sublanes = 8
everyone = ("seq", "batch")
f32 = jnp.float32
bf16 = jnp.bfloat16


def rows_of(ref, seq, block):
    return ref[seq, pl.ds(pl.multiple_of(block * sublanes, sublanes), sublanes), :]


def spread(rows, index, count):
    return jnp.broadcast_to(rows[index : index + 1], (count, lanes))


def encode_kernel(reverse, input_ref, decay_ref, end_ref):
    seq_count, step_count, _ = input_ref.shape
    state_count = decay_ref.shape[0]
    blocks = step_count // sublanes
    power = jnp.exp(-decay_ref[...])

    def one_block(step, states):
        block = blocks - 1 - step if reverse else step
        rows = [rows_of(input_ref, seq, block) for seq in range(seq_count)]
        order = range(sublanes - 1, -1, -1) if reverse else range(sublanes)
        states = list(states)
        for index in order:
            for seq in range(seq_count):
                states[seq] = states[seq] * power + spread(rows[seq], index, state_count)
        return tuple(states)

    start = tuple(jnp.zeros((state_count, lanes), f32) for _ in range(seq_count))
    ends = lax.fori_loop(0, blocks, one_block, start)
    for seq in range(seq_count):
        end_ref[seq] = ends[seq]


def output_kernel(input_ref, query_ref, carried_ref, decay_ref, weight_ref, skip_ref, out_ref, gated_ref):
    seq_count, step_count, _ = input_ref.shape
    state_count = decay_ref.shape[0]
    power = jnp.exp(-decay_ref[...])
    weight = weight_ref[...]
    skip = skip_ref[...]

    def one_block(block, states):
        states = list(states)
        rows = [rows_of(input_ref, seq, block) for seq in range(seq_count)]
        found = [[] for _ in range(seq_count)]
        for index in range(sublanes):
            for seq in range(seq_count):
                states[seq] = states[seq] * power + spread(rows[seq], index, state_count)
                found[seq].append(jnp.sum(states[seq] * weight, axis=0, keepdims=True))
        place = pl.ds(pl.multiple_of(block * sublanes, sublanes), sublanes)
        for seq in range(seq_count):
            result = jnp.concatenate(found[seq], axis=0) + skip * rows[seq]
            out_ref[seq, place, :] = result
            gated_ref[seq, place, :] = result * rows_of(query_ref, seq, block)
        return tuple(states)

    start = tuple(carried_ref[seq].astype(f32) for seq in range(seq_count))
    lax.fori_loop(0, step_count // sublanes, one_block, start)


def back_kernel(
    input_ref,
    grad_ref,
    carried_ref,
    later_ref,
    decay_ref,
    weight_ref,
    skip_ref,
    input_grad_ref,
    weight_grad_ref,
    power_grad_ref,
    skip_grad_ref,
    held,
):
    seq_count, step_count, _ = input_ref.shape
    state_count = decay_ref.shape[0]
    blocks = step_count // sublanes
    power = jnp.exp(-decay_ref[...])
    weight = weight_ref[...]
    skip = skip_ref[...]
    seqs = range(seq_count)

    def forward_block(block, state):
        states, total, skip_total = list(state[0]), state[1], state[2]
        rows = [rows_of(input_ref, seq, block) for seq in seqs]
        grads = [rows_of(grad_ref, seq, block) for seq in seqs]
        for index in range(sublanes):
            for seq in seqs:
                held[block * sublanes + index, seq] = states[seq]
                states[seq] = states[seq] * power + spread(rows[seq], index, state_count)
                total = total + states[seq] * spread(grads[seq], index, state_count)
        for seq in seqs:
            skip_total = skip_total + rows[seq] * grads[seq]
        return (tuple(states), total, skip_total)

    zeros = jnp.zeros((state_count, lanes), f32)
    _, total, skip_total = lax.fori_loop(
        0,
        blocks,
        forward_block,
        (
            tuple(carried_ref[seq].astype(f32) for seq in seqs),
            zeros,
            jnp.zeros((sublanes, lanes), f32),
        ),
    )
    weight_grad_ref[...] = total
    skip_grad_ref[...] = jnp.sum(skip_total, axis=0, keepdims=True)

    def back_block(step, state):
        states, total = list(state[0]), state[1]
        block = blocks - 1 - step
        grads = [rows_of(grad_ref, seq, block) for seq in seqs]
        found = [[None] * sublanes for _ in seqs]
        for index in range(sublanes - 1, -1, -1):
            for seq in seqs:
                states[seq] = states[seq] * power + spread(grads[seq], index, state_count)
                found[seq][index] = jnp.sum(states[seq] * weight, axis=0, keepdims=True)
                total = total + states[seq] * held[block * sublanes + index, seq]
        place = pl.ds(pl.multiple_of(block * sublanes, sublanes), sublanes)
        for seq in seqs:
            input_grad_ref[seq, place, :] = jnp.concatenate(found[seq], axis=0) + skip * grads[seq]
        return (tuple(states), total)

    _, total = lax.fori_loop(
        0, blocks, back_block, (tuple(later_ref[seq].astype(f32) for seq in seqs), zeros)
    )
    power_grad_ref[...] = total * weight


def per_lane_tile(kernel, args, outs, scratch=(), flops=0):
    def spec(shape):
        lead = len(shape) - 1
        return pl.BlockSpec(tuple(shape[:-1]) + (lanes,), lambda tile: (0,) * lead + (tile,))

    bytes_moved = sum(a.size * a.dtype.itemsize for a in args)
    return pl.pallas_call(
        kernel,
        grid=(args[0].shape[-1] // lanes,),
        in_specs=[spec(a.shape) for a in args],
        out_specs=[spec(o.shape) for o in outs],
        out_shape=list(outs),
        scratch_shapes=list(scratch),
        cost_estimate=pl.CostEstimate(flops=flops, bytes_accessed=bytes_moved, transcendentals=0),
        compiler_params=pltpu.CompilerParams(vmem_limit_bytes=48 * 1024 * 1024),
    )(*args)


def shaped(*dims, dtype=f32):
    return jax.ShapeDtypeStruct(dims, dtype)


def encode(value, decay, reverse):
    seq_count, _, width = value.shape
    (ends,) = per_lane_tile(
        functools.partial(encode_kernel, reverse),
        (value, decay),
        (shaped(seq_count, decay.shape[0], width),),
    )
    return ends


def passed_along(block, axis, distance):
    devices = range(lax.axis_size(axis))
    route = [(i - distance, i) for i in devices if i - distance in devices]
    return lax.ppermute(block, axis, route)


def carried_in(ends, block_power, direction):
    count = lax.axis_size("seq")
    carried = passed_along(ends.astype(bf16), "seq", direction).astype(f32)
    distance = 1
    while distance < count - 1:
        arrived = passed_along(carried.astype(bf16), "seq", direction * distance).astype(f32)
        carried = carried + jnp.power(block_power, distance)[None] * arrived
        distance *= 2
    return carried


def split_heads(ref, scratch, heads, parts, first=0):
    for part in range(parts):
        for head in range(heads):
            start = (part * heads + head) * HEAD_DIM + first
            scratch[part * heads + head] = ref[:, start : start + HEAD_DIM]


def score_block(query, keys, first, scale):
    scores = (
        lax.dot_general(query, keys, (((1,), (1,)), ((), ())), preferred_element_type=f32) * scale
    )
    rows = lax.broadcasted_iota(jnp.int32, scores.shape, 0) + first
    columns = lax.broadcasted_iota(jnp.int32, scores.shape, 1)
    return jnp.where(columns <= rows, scores, masked_score)


def attend_kernel(heads, block, scale, qkv_ref, low_ref, full_ref, stat_ref, parts, outs):
    length = qkv_ref.shape[0]
    split_heads(qkv_ref, parts, heads, 3)

    @pl.loop(0, heads)
    def _(head):
        for first in range(0, length, block):
            extent = first + block
            query = parts[head, first:extent, :]
            scores = score_block(query, parts[heads + head, :extent, :], first, scale)
            top = jnp.max(scores, axis=1, keepdims=True)
            soft = jnp.exp(scores - top)
            whole = jnp.sum(soft, axis=1, keepdims=True)
            soft = soft * (1.0 / whole)
            outs[head, first:extent, :] = jnp.dot(
                soft.astype(bf16), parts[2 * heads + head, :extent, :], preferred_element_type=f32
            )
            stat_ref[head, first:extent, :] = jnp.broadcast_to(top + jnp.log(whole), (block, lanes))

    for head in range(heads):
        place = slice(head * HEAD_DIM, (head + 1) * HEAD_DIM)
        full_ref[:, place] = outs[head]
        low_ref[:, place] = outs[head].astype(bf16)


def attend_back_kernel(
    heads, block, scale, qkv_ref, dout_ref, full_ref, stat_ref, grad_ref, parts, douts, fulls, grads
):
    length = qkv_ref.shape[0]
    split_heads(qkv_ref, parts, heads, 3)
    split_heads(dout_ref, douts, heads, 1)
    split_heads(full_ref, fulls, heads, 1)
    grads[...] = jnp.zeros_like(grads)

    @pl.loop(0, heads)
    def _(head):
        for first in range(0, length, block):
            extent = first + block
            query = parts[head, first:extent, :]
            keys = parts[heads + head, :extent, :]
            value = parts[2 * heads + head, :extent, :]
            dout = douts[head, first:extent, :]
            delta = jnp.sum(dout.astype(f32) * fulls[head, first:extent, :], axis=1, keepdims=True)
            scores = score_block(query, keys, first, scale)
            soft = jnp.exp(scores - stat_ref[head, first:extent, :1])
            across = (((1,), (1,)), ((), ()))
            along = (((0,), (0,)), ((), ()))
            dprob = lax.dot_general(dout, value, across, preferred_element_type=f32)
            dscore = (soft * (dprob - delta) * scale).astype(bf16)
            grads[head, first:extent, :] = jnp.dot(dscore, keys, preferred_element_type=f32)
            grads[heads + head, :extent, :] += lax.dot_general(
                dscore, query, along, preferred_element_type=f32
            )
            grads[2 * heads + head, :extent, :] += lax.dot_general(
                soft.astype(bf16), dout, along, preferred_element_type=f32
            )

    grad_ref[...] = jnp.zeros_like(grad_ref)
    for part in range(3 * heads):
        grad_ref[:, part * HEAD_DIM : (part + 1) * HEAD_DIM] = grads[part].astype(bf16)


def attend_params():
    return pltpu.CompilerParams(vmem_limit_bytes=56 * 1024 * 1024)


def attend_whole(qkv, heads, block):
    length = qkv.shape[0]
    width = heads * HEAD_DIM
    return pl.pallas_call(
        functools.partial(attend_kernel, heads, block, HEAD_DIM ** (-0.5)),
        out_shape=[
            shaped(length, width, dtype=bf16),
            shaped(length, width),
            shaped(heads, length, lanes),
        ],
        scratch_shapes=[
            pltpu.VMEM((3 * heads, length, HEAD_DIM), bf16),
            pltpu.VMEM((heads, length, HEAD_DIM), f32),
        ],
        compiler_params=attend_params(),
    )(qkv)


def attend_whole_back(qkv, dout, full, stat, heads, block):
    length = qkv.shape[0]
    return pl.pallas_call(
        functools.partial(attend_back_kernel, heads, block, HEAD_DIM ** (-0.5)),
        out_shape=shaped(*qkv.shape, dtype=bf16),
        scratch_shapes=[
            pltpu.VMEM((3 * heads, length, HEAD_DIM), bf16),
            pltpu.VMEM((heads, length, HEAD_DIM), bf16),
            pltpu.VMEM((heads, length, HEAD_DIM), f32),
            pltpu.VMEM((3 * heads, length, HEAD_DIM), f32),
        ],
        compiler_params=attend_params(),
    )(qkv, dout, full, stat)


def split_blocks(array, block_len):
    shaped_blocks = array.reshape(
        (array.shape[0], array.shape[1] // block_len, block_len) + array.shape[2:]
    )
    return jnp.moveaxis(shaped_blocks, 1, 0)


def general_attention(proj_low, seq_count, block_len, places, any_live, longest):
    model_width = HEADS * HEAD_DIM
    scale = HEAD_DIM ** (-0.5)
    offsets = jnp.arange(block_len, dtype=jnp.int32)
    head_shape = (seq_count, block_len, HEADS, HEAD_DIM)
    query_low = proj_low[:, :model_width].reshape(head_shape)
    keys_low = proj_low[:, model_width : 2 * model_width].reshape(head_shape)
    value_low = proj_low[:, 2 * model_width :].reshape(head_shape)

    def block_scores(queries, keys_block, query_places, key_places):
        scores = (
            jnp.einsum("sqhe,skhe->sqhk", queries, keys_block, preferred_element_type=jnp.float32)
            * scale
        )
        causal_mask = key_places[None, :] <= query_places[:, None]
        return jnp.where(causal_mask[None, :, None, :], scores, masked_score)

    def key_needed(key_first):
        return (key_first <= places[-1]) & ((key_first == places[0]) | any_live)

    stat_shape = (seq_count, block_len, HEADS)
    start_state = (
        jnp.full(stat_shape, masked_score, jnp.float32),
        jnp.zeros(stat_shape, jnp.float32),
        jnp.zeros(head_shape, jnp.float32),
    )
    shard_piece = (
        lax.all_gather(keys_low, "seq", axis=1, tiled=True),
        lax.all_gather(value_low, "seq", axis=1, tiled=True),
    )
    keys_blocks = split_blocks(shard_piece[0], block_len)
    value_blocks = split_blocks(shard_piece[1], block_len)
    firsts = jnp.arange(keys_blocks.shape[0], dtype=jnp.int32) * block_len

    def attend_one_step(state_now, operand):
        keys_block, value_block, key_first = operand

        def attend_work(state_in_block):
            running_max, running_sum, running_out = state_in_block
            scores = block_scores(query_low, keys_block, places, key_first + offsets)
            new_max = jnp.maximum(running_max, jnp.max(scores, axis=-1))
            fade = jnp.exp(running_max - new_max)
            shifted = jnp.exp(scores - new_max[..., None])
            new_sum = running_sum * fade + jnp.sum(shifted, axis=-1)
            new_out = running_out * fade[..., None] + jnp.einsum(
                "sqhk,skhe->sqhe",
                shifted.astype(jnp.bfloat16),
                value_block,
                preferred_element_type=jnp.float32,
            )
            return (new_max, new_sum, new_out)

        return (
            lax.cond(
                key_needed(key_first), attend_work, lambda state_in_block: state_in_block, state_now
            ),
            None,
        )

    result, _ = lax.scan(attend_one_step, start_state, (keys_blocks, value_blocks, firsts))
    running_max, running_sum, running_out = result
    attended = running_out / running_sum[..., None]
    logsum = running_max + jnp.log(running_sum)
    def backward(dout_low):
        delta = jnp.sum(dout_low.astype(jnp.float32) * attended, axis=-1)
        shard_piece = (
            lax.all_gather(keys_low, "seq", axis=1, tiled=True),
            lax.all_gather(value_low, "seq", axis=1, tiled=True),
        )
        keys_blocks = split_blocks(shard_piece[0], block_len)
        value_blocks = split_blocks(shard_piece[1], block_len)
        firsts = jnp.arange(keys_blocks.shape[0], dtype=jnp.int32) * block_len

        def query_one_step(query_grad, operand):
            keys_block, value_block, key_first = operand

            def query_work(grad_now):
                scores = block_scores(query_low, keys_block, places, key_first + offsets)
                soft = jnp.exp(scores - logsum[..., None])
                dprob = jnp.einsum(
                    "sqhe,skhe->sqhk", dout_low, value_block, preferred_element_type=jnp.float32
                )
                dscore = (soft * (dprob - delta[..., None])).astype(jnp.bfloat16)
                return (
                    grad_now
                    + jnp.einsum(
                        "sqhk,skhe->sqhe", dscore, keys_block, preferred_element_type=jnp.float32
                    )
                    * scale
                )

            return (
                lax.cond(key_needed(key_first), query_work, lambda grad_now: grad_now, query_grad),
                None,
            )

        result, _ = lax.scan(
            query_one_step, jnp.zeros(head_shape, jnp.float32), (keys_blocks, value_blocks, firsts)
        )
        query_grad = result
        sent = (query_low.astype(jnp.float32), dout_low.astype(jnp.float32), logsum, delta)
        shard_piece = (
            lax.all_gather(sent[0].astype(jnp.bfloat16), "seq", axis=1, tiled=True).astype(jnp.float32),
            lax.all_gather(sent[1].astype(jnp.bfloat16), "seq", axis=1, tiled=True).astype(jnp.float32),
            lax.all_gather(sent[2].astype(jnp.bfloat16), "seq", axis=1, tiled=True).astype(jnp.float32),
            lax.all_gather(sent[3].astype(jnp.bfloat16), "seq", axis=1, tiled=True).astype(jnp.float32),
        )
        query_blocks = split_blocks(shard_piece[0], block_len)
        dout_blocks = split_blocks(shard_piece[1], block_len)
        logsum_blocks = split_blocks(shard_piece[2], block_len)
        delta_blocks = split_blocks(shard_piece[3], block_len)
        firsts = jnp.arange(query_blocks.shape[0], dtype=jnp.int32) * block_len

        def key_one_step(grads_now, operand):
            query_block, dout_block, logsum_block, delta_block, query_first = operand

            def key_work(grads_in):
                keys_grad, value_grad = grads_in
                query_cast = query_block.astype(jnp.bfloat16)
                dout_cast = dout_block.astype(jnp.bfloat16)
                scores = block_scores(query_cast, keys_low, query_first + offsets, places)
                soft = jnp.exp(scores - logsum_block[..., None])
                value_grad = value_grad + jnp.einsum(
                    "sqhk,sqhe->skhe",
                    soft.astype(jnp.bfloat16),
                    dout_cast,
                    preferred_element_type=jnp.float32,
                )
                dprob = jnp.einsum(
                    "sqhe,skhe->sqhk", dout_cast, value_low, preferred_element_type=jnp.float32
                )
                dscore = (soft * (dprob - delta_block[..., None])).astype(jnp.bfloat16)
                keys_grad = (
                    keys_grad
                    + jnp.einsum(
                        "sqhk,sqhe->skhe", dscore, query_cast, preferred_element_type=jnp.float32
                    )
                    * scale
                )
                return (keys_grad, value_grad)

            needed = (query_first + block_len - 1 >= places[0]) & (
                (query_first == places[0]) | (query_first < longest)
            )
            return (lax.cond(needed, key_work, lambda grads_in: grads_in, grads_now), None)

        result, _ = lax.scan(
            key_one_step,
            (jnp.zeros(head_shape, jnp.float32), jnp.zeros(head_shape, jnp.float32)),
            (query_blocks, dout_blocks, logsum_blocks, delta_blocks, firsts),
        )
        keys_grad, value_grad = result
        return (query_grad, keys_grad, value_grad)

    return attended, backward


def layer_norm(value, gain):
    centred = value - jnp.mean(value, axis=-1, keepdims=True)
    spread_of = jnp.mean(centred * centred, axis=-1, keepdims=True)
    return centred * lax.rsqrt(spread_of + eps) * gain


def gelu_tanh(value):
    return jax.nn.gelu(value, approximate=True)


def dense(left, weight):
    return jnp.dot(left, weight, preferred_element_type=f32)


def dense_back(left, weight, upstream):
    into_left = lax.dot_general(
        upstream, weight, (((1,), (1,)), ((), ())), preferred_element_type=f32
    )
    into_weight = lax.dot_general(
        left, upstream, (((0,), (0,)), ((), ())), preferred_element_type=f32
    ).astype(bf16)
    return (into_left, into_weight)


def shift_mix(extended, taps, value_part):
    step_count = value_part.shape[1]
    reach = taps.shape[1]
    shifted = extended[:, reach - 1 : reach - 1 + step_count] * taps[:, 0]
    for tap_index in range(1, reach):
        shifted = (
            shifted
            + extended[:, reach - 1 - tap_index : reach - 1 - tap_index + step_count]
            * taps[:, tap_index]
        )
    return shifted * value_part


def feed_forward(resid, gain, up_weight, down_weight):
    normed, norm_back = jax.vjp(layer_norm, resid, gain)
    normed_low = normed.astype(bf16)
    hidden = dense(normed_low, up_weight)
    active, active_back = jax.vjp(gelu_tanh, hidden)
    active_low = active.astype(bf16)
    return (
        resid + dense(active_low, down_weight),
        (norm_back, normed_low, active_back, active_low),
    )


def feed_back(stored, up_weight, down_weight, upstream):
    norm_back, normed_low, active_back, active_low = stored
    into_active, down_grad = dense_back(active_low, down_weight, upstream.astype(bf16))
    (into_hidden,) = active_back(into_active)
    into_normed, up_grad = dense_back(normed_low, up_weight, into_hidden.astype(bf16))
    into_resid, gain_grad = norm_back(into_normed)
    return (upstream + into_resid, gain_grad, up_grad, down_grad)


def fold_rows(weight, share):
    rows, width = weight.shape
    fold = rows // share
    return weight.reshape(fold, share, width).transpose(1, 0, 2).reshape(share, fold * width)


def unfold_rows(folded, fold, share):
    rows, width = folded.shape
    width //= fold
    parts = folded.reshape(rows // share, share, fold, width).transpose(0, 2, 1, 3)
    return parts.reshape(rows * fold, width)


def fold_all(weight, share, rows):
    tall, width = weight.shape
    fold = tall // rows
    parts = weight.reshape(rows // share, fold, share, width).transpose(0, 2, 1, 3)
    return parts.reshape(rows, fold * width)


def group_columns(weight, groups, padded):
    rows, columns = weight.shape
    part = columns // 3 // groups
    grouped = weight.reshape(rows, 3, groups, part).transpose(0, 2, 1, 3).reshape(rows, groups, 3 * part)
    return jnp.pad(grouped, ((0, 0), (0, 0), (0, padded - 3 * part))).reshape(rows, groups * padded)


def ungroup_columns(grouped, groups, padded, columns):
    rows = grouped.shape[0]
    part = columns // 3 // groups
    parts = grouped.reshape(rows, groups, padded)[:, :, : 3 * part].reshape(rows, groups, 3, part)
    return parts.transpose(0, 2, 1, 3).reshape(rows, columns)


def cut(array, widths):
    pieces, start = [], 0
    for width in widths:
        pieces.append(array[:, start : start + width])
        start += width
    return pieces


def gathered(parts):
    whole = lax.all_gather(jnp.concatenate(parts, axis=1), everyone, axis=0, tiled=True)
    return cut(whole, [p.shape[1] for p in parts])


def scattered(parts):
    mine = lax.psum_scatter(
        jnp.concatenate(parts, axis=1), everyone, scatter_dimension=0, tiled=True
    )
    return cut(mine, [p.shape[1] for p in parts])


def body(
    tokens,
    cotangent,
    lengths,
    mixer_gain,
    mixer_inputs,
    shift_taps,
    decay_rate,
    state_in,
    state_out,
    state_skip,
    mixer_output,
    first_gain,
    first_up,
    first_down,
    attend_gain,
    attend_inputs,
    attend_output,
    second_gain,
    second_up,
    second_down,
):
    seq_count, block_len, model_width = tokens.shape
    row_count = seq_count * block_len
    seq_devices = lax.axis_size("seq")
    share = mixer_inputs.shape[0]
    states, reach = decay_rate.shape[1], shift_taps.shape[1]
    fold = first_down.shape[0] // share
    deals = seq_count * HEADS
    dealt = deals % seq_devices == 0 and HEADS % (deals // seq_devices) == 0
    heads = deals // seq_devices if dealt else HEADS
    groups = HEADS // heads
    group_width = heads * HEAD_DIM
    padded = -(-3 * group_width // lanes) * lanes if dealt else 3 * group_width

    columns = [decay_rate, state_in, state_out, shift_taps]
    columns += [g[:, None] for g in (mixer_gain, first_gain, attend_gain, second_gain, state_skip)]
    small = jnp.concatenate(columns, axis=1)
    small_count = small.shape[1]
    small_width = -(-small_count // lanes) * lanes
    small = jnp.pad(small, ((0, 0), (0, small_width - small_count)))
    w_mixer_in, w_small = gathered([mixer_inputs, small])
    attend_cols = attend_inputs.shape[1]
    w_mixer_out, w_up1, w_down1, w_attend_in, w_attend_out, w_up2, w_down2 = gathered(
        [
            mixer_output,
            first_up,
            fold_rows(first_down, share),
            group_columns(attend_inputs, groups, padded),
            attend_output,
            second_up,
            fold_rows(second_down, share),
        ]
    )
    w_down1 = unfold_rows(w_down1, fold, share)
    w_down2 = unfold_rows(w_down2, fold, share)

    rows = w_small.T.astype(f32)
    decay, table_in, table_out = rows[:states], rows[states : 2 * states], rows[2 * states : 3 * states]
    taps_rows = rows[3 * states : 3 * states + reach]
    gain_mixer, gain_first, gain_attend, gain_second, skip = (
        rows[3 * states + reach + i] for i in range(5)
    )
    taps = taps_rows.T
    weight = table_in * table_out

    rank_seq = lax.axis_index("seq")
    offsets = jnp.arange(block_len, dtype=jnp.int32)
    places = rank_seq * block_len + offsets
    valid = (places[None, :] < lengths[:, None]).astype(f32)
    longest = jnp.max(lengths)
    any_live = places[0] < longest

    start_resid = tokens.reshape(row_count, model_width).astype(f32)
    normed_mixer, back_mixer = jax.vjp(layer_norm, start_resid, gain_mixer)
    normed_low_mixer = normed_mixer.astype(bf16)
    projected = dense(normed_low_mixer, w_mixer_in).reshape(seq_count, block_len, 3 * model_width)
    query_mixer = projected[:, :, :model_width]
    keys_mixer = projected[:, :, model_width : 2 * model_width]
    value_mixer = projected[:, :, 2 * model_width :]
    rim_rows = passed_along(keys_mixer[:, block_len - reach + 1 :], "seq", 1)
    extended = jnp.concatenate([rim_rows, keys_mixer], axis=1)
    inner, shift_back = jax.vjp(shift_mix, extended, taps, value_mixer)
    block_power = jnp.exp(-decay * block_len)
    ends = encode(inner, decay, False)
    carried = carried_in(ends, block_power, 1)
    wide = shaped(seq_count, block_len, model_width)
    state_y, gated = per_lane_tile(
        output_kernel,
        (inner, query_mixer, carried, decay, weight, skip[None]),
        (wide, wide),
    )
    gated_low = gated.astype(bf16).reshape(row_count, model_width)
    resid_mixer = start_resid + dense(gated_low, w_mixer_out)
    resid_first, stored_first = feed_forward(resid_mixer, gain_first, w_up1, w_down1)

    normed_attend, back_attend = jax.vjp(layer_norm, resid_first, gain_attend)
    normed_low_attend = normed_attend.astype(bf16)
    proj_low = dense(normed_low_attend, w_attend_in).astype(bf16)
    if dealt:
        length = seq_devices * block_len
        block = min(256, length)

        def deal(array, width):
            parts = array.reshape(seq_count, block_len, groups, width).transpose(0, 2, 1, 3)
            parts = parts.reshape(seq_count * groups, block_len, width)
            dealt_parts = lax.all_to_all(parts, "seq", split_axis=0, concat_axis=0, tiled=True)
            return dealt_parts.reshape(length, width)

        def collect(array, width):
            parts = array.reshape(seq_devices, block_len, width)
            back = lax.all_to_all(parts, "seq", split_axis=0, concat_axis=0, tiled=True)
            back = back.reshape(seq_count, groups, block_len, width).transpose(0, 2, 1, 3)
            return back.reshape(row_count, groups * width)

        qkv = deal(proj_low, padded)
        attended_part, attended_full, stat = attend_whole(qkv, heads, block)
        attended_low = collect(attended_part, group_width)
    else:
        attended, attended_back = general_attention(
            proj_low, seq_count, block_len, places, any_live, longest
        )
        attended_low = attended.reshape(row_count, model_width).astype(bf16)
    resid_attend = resid_first + dense(attended_low, w_attend_out)
    final, stored_second = feed_forward(resid_attend, gain_second, w_up2, w_down2)
    mixed = (final.reshape(seq_count, block_len, model_width) * valid[..., None]).astype(bf16)

    upstream = (cotangent.astype(f32) * valid[..., None]).reshape(row_count, model_width)
    upstream, second_gain_grad, second_up_grad, second_down_grad = feed_back(
        stored_second, w_up2, w_down2, upstream
    )
    into_attended, attend_output_grad = dense_back(
        attended_low, w_attend_out, upstream.astype(bf16)
    )
    second_up_out, second_down_out, attend_output_out = scattered(
        [second_up_grad, fold_all(second_down_grad, share, model_width), attend_output_grad]
    )
    dout_low = into_attended.astype(bf16)
    if dealt:
        dout = deal(dout_low, group_width)
        proj_grad = collect(
            attend_whole_back(qkv, dout, attended_full, stat, heads, block), padded
        )
    else:
        parts = attended_back(dout_low.reshape(seq_count, block_len, HEADS, HEAD_DIM))
        proj_grad = jnp.concatenate(
            [p.reshape(row_count, model_width) for p in parts], axis=1
        ).astype(bf16)
    into_normed, attend_inputs_grad = dense_back(normed_low_attend, w_attend_in, proj_grad)
    into_resid, attend_gain_grad = back_attend(into_normed)
    upstream = upstream + into_resid
    upstream, first_gain_grad, first_up_grad, first_down_grad = feed_back(
        stored_first, w_up1, w_down1, upstream
    )
    into_gated, mixer_output_grad = dense_back(gated_low, w_mixer_out, upstream.astype(bf16))
    into_gated = into_gated.reshape(seq_count, block_len, model_width)
    query_mixer_grad = into_gated * state_y
    state_grad = into_gated * query_mixer
    later = carried_in(encode(state_grad, decay, True), block_power, -1)
    table = shaped(states, model_width)
    inner_grad, weight_grad, power_grad, skip_grad = per_lane_tile(
        back_kernel,
        (inner, state_grad, carried, later, decay, weight, skip[None]),
        (wide, table, table, shaped(1, model_width)),
        scratch=[pltpu.VMEM((block_len, seq_count, states, lanes), f32)],
    )
    extended_grad, taps_grad, value_mixer_grad = shift_back(inner_grad)
    spill = passed_along(extended_grad[:, : reach - 1], "seq", -1)
    keys_mixer_grad = extended_grad[:, reach - 1 :] + jnp.pad(
        spill, ((0, 0), (block_len - reach + 1, 0), (0, 0))
    )
    proj_grad_mixer = (
        jnp.concatenate([query_mixer_grad, keys_mixer_grad, value_mixer_grad], axis=2)
        .astype(bf16)
        .reshape(row_count, 3 * model_width)
    )
    into_normed_mixer, mixer_inputs_grad = dense_back(normed_low_mixer, w_mixer_in, proj_grad_mixer)
    into_start, mixer_gain_grad = back_mixer(into_normed_mixer)
    tokens_gradient = (upstream + into_start).reshape(seq_count, block_len, model_width).astype(bf16)

    small_rows = jnp.concatenate(
        [-jnp.exp(-decay) * power_grad, weight_grad * table_out, weight_grad * table_in, taps_grad.T]
        + [
            g[None]
            for g in (mixer_gain_grad, first_gain_grad, attend_gain_grad, second_gain_grad, skip_grad[0])
        ],
        axis=0,
    )
    small_grad = jnp.pad(small_rows, ((0, small_width - small_count), (0, 0))).T.astype(bf16)
    attend_inputs_out, first_up_out, first_down_out, mixer_output_out, mixer_inputs_out, small_out = scattered(
        [
            attend_inputs_grad,
            first_up_grad,
            fold_all(first_down_grad, share, model_width),
            mixer_output_grad,
            mixer_inputs_grad,
            small_grad,
        ]
    )
    small_out = small_out.astype(f32)
    gains_at = 3 * states + reach

    def unfolded(folded):
        return folded.reshape(share, fold, model_width).transpose(1, 0, 2).reshape(share * fold, model_width)

    return (
        mixed,
        tokens_gradient,
        small_out[:, gains_at],
        mixer_inputs_out.astype(f32),
        small_out[:, 3 * states : gains_at],
        small_out[:, :states],
        small_out[:, states : 2 * states],
        small_out[:, 2 * states : 3 * states],
        small_out[:, gains_at + 4],
        mixer_output_out.astype(f32),
        small_out[:, gains_at + 1],
        first_up_out.astype(f32),
        unfolded(first_down_out).astype(f32),
        small_out[:, gains_at + 2],
        ungroup_columns(attend_inputs_out, groups, padded, attend_cols).astype(f32),
        attend_output_out.astype(f32),
        small_out[:, gains_at + 3],
        second_up_out.astype(f32),
        unfolded(second_down_out).astype(f32),
    )


def solution(mesh):
    return jax.shard_map(
        body,
        mesh=mesh,
        in_specs=(
            P("batch", "seq", None),
            P("batch", "seq", None),
            P("batch"),
            P(("seq", "batch")),
            P(("seq", "batch"), None),
            P(("seq", "batch"), None),
            P(("seq", "batch"), None),
            P(("seq", "batch"), None),
            P(("seq", "batch"), None),
            P(("seq", "batch")),
            P(("seq", "batch"), None),
            P(("seq", "batch")),
            P(("seq", "batch"), None),
            P(("seq", "batch"), None),
            P(("seq", "batch")),
            P(("seq", "batch"), None),
            P(("seq", "batch"), None),
            P(("seq", "batch")),
            P(("seq", "batch"), None),
            P(("seq", "batch"), None),
        ),
        out_specs=(
            P("batch", "seq", None),
            P("batch", "seq", None),
            P(("seq", "batch")),
            P(("seq", "batch"), None),
            P(("seq", "batch"), None),
            P(("seq", "batch"), None),
            P(("seq", "batch"), None),
            P(("seq", "batch"), None),
            P(("seq", "batch")),
            P(("seq", "batch"), None),
            P(("seq", "batch")),
            P(("seq", "batch"), None),
            P(("seq", "batch"), None),
            P(("seq", "batch")),
            P(("seq", "batch"), None),
            P(("seq", "batch"), None),
            P(("seq", "batch")),
            P(("seq", "batch"), None),
            P(("seq", "batch"), None),
        ),
        check_vma=False,
    )
```

time: 4430 us -> 837 us (0.19)
  local copies, waits for them, and re-layouts: 1070 us -> 96.4 us
  waiting for transfers between devices: 1290 us -> 445 us
  other arithmetic: 802 us -> 32.7 us
  matrix products: 784 us -> 66.9 us
  blocking collectives: 366 us -> 52.3 us
  loops' own time: 74.6 us -> 0 us
  Pallas kernels: 0 us -> 61.1 us
  starting transfers between devices: 3.8 us -> 60.5 us
    reduce_scatter x8 -> x2, waiting for transfers between devices: 920 us -> 204 us  [scattered(): lax.psum_scatter(jnp.concatenate(parts, axis=1), everyone, scatter_dimens...]
    dot_general x84 -> x8, matrix products: 727 us -> 24.8 us  [dense(): return jnp.dot(left, weight, preferred_element_type=f32)]
    scatter-add x6 -> x0, other arithmetic: 590 us -> none  [one_group(): toeplitz = jnp.where(causal_mask, kernel[lag_index], 0.0)]
    dynamic_update_slice x66 -> x0, local copies, waits for them, and re-layouts: 386 us -> none  [state_output(): lax.map(one_group, (split_groups(inner), split_states(carried), split_par...]
    gather x12 -> x0, local copies, waits for them, and re-layouts: 383 us -> none  [one_group(): toeplitz = jnp.where(causal_mask, kernel[lag_index], 0.0)]
    all_gather x7 -> x0, blocking collectives: 242 us -> none  [the longest x1 41 us: body(): lax.all_gather(shards[2], ('seq', 'batch'), axis=0, tiled=True)]
    all_gather x14 -> x2, waiting for transfers between devices: 284 us -> 141 us  [gathered(): lax.all_gather(jnp.concatenate(parts, axis=1), everyone, axis=0, tiled=True)]
    unnamed x2 -> x0, blocking collectives: 124 us -> none
  transfers between devices with their start and end apart: 27 -> 16, of which waited for: 14 -> 13; matrix products, arithmetic and copies ran while one was open for 34% -> 11% of each run, Pallas kernels for 0% -> 6%
where the time goes in v1:
time: 837 us; the launch traced here: 831 us
  waiting for transfers between devices  445 us (53%)
  local copies, waits for them, and re-layouts  96.4 us (12%)
  matrix products  66.9 us (8%)
  Pallas kernels  61.1 us (7%)
  starting transfers between devices  60.5 us (7%)
  blocking collectives  52.3 us (6%)
  other arithmetic  32.7 us (4%)
  between operations  15.9 us (2%)
    reduce_scatter x2, waiting for transfers between devices, scattered(): lax.psum_scatter(jnp.concatenate(parts, axis=1), everyone, scatter_dimens...  204 us
    all_gather x2, waiting for transfers between devices, gathered(): lax.all_gather(jnp.concatenate(parts, axis=1), everyone, axis=0, tiled=True)  141 us
    all_to_all x2, waiting for transfers between devices, collect(): back = lax.all_to_all(parts, 'seq', split_axis=0, concat_axis=0, tiled=True)  53.1 us
    all_to_all x2, blocking collectives, deal(): lax.all_to_all(parts, 'seq', split_axis=0, concat_axis=0, tiled=True)  52.3 us
    ppermute x10, starting transfers between devices, passed_along(): return lax.ppermute(block, axis, route)  51.8 us
    ppermute x10, waiting for transfers between devices, passed_along(): return lax.ppermute(block, axis, route)  47.3 us
    pallas_call x4, Pallas kernels, per_lane_tile(): pl.pallas_call(kernel, grid=(args[0].shape[-1] // lanes,), in_specs=[spec...  37.6 us
    dot_general x8, matrix products, dense_back(): lax.dot_general(upstream, weight, (((1,), (1,)), ((), ())), preferred_ele...  25.1 us
  transfers between devices with their start and end apart: 16, of which 13 were waited for; matrix products, arithmetic and copies ran while one was open for 11% of the time, Pallas kernels for 6%

profile of v1, /device:TPU:0, one launch (start us, length us, event | category | flops | bytes accessed | tf_op | source)
XLA Modules:
  0.0 830.7 jit_solution(9877228161383919477)
XLA Ops:
  21.1 57.0 %all-gather.3.cloned.1.call-done = bf16[768,2560]{1,0:T(8,128)(2,1)} async-done(((bf16[24,2560]{1,0:T(8,128)(2,1)}), bf16[768,2560]{1,0:T(8,128)(2,1)}) %all-gather.3.cloned.1.call-update) | async-done | bytes 3932176 | tf_op jit(solution)/shard_map/all_gather | solution.py:577
  100.8 9.6 %collective-permute-start.2 = (bf16[2,64,768]{2,1,0:T(8,128)(2,1)S(1)}, bf16[2,64,768]{2,1,0:T(8,128)(2,1)S(1)}, u32[]{:S(2)}, u32[]{:S(2)}) collective-permute-start(bf16[2,64,768]{2,1,0:T(8,128)(2,1)S(1)} %collective-permute-done.1), channel_id=1, source_target_pairs={{0,4},{4,8},{8,12},{12,16},{16,20},{20,24},{24,28},{1,5},{5,9},{9,... | collective-permute-start | bytes 589832 | tf_op jit(solution)/shard_map/ppermute | solution.py:183
  113.6 7.2 collective-permute-start.3
  120.8 8.1 collective-permute-done.3
  129.0 20.0 %collective-permute-start.4 = (bf16[2,64,768]{2,1,0:T(8,128)(2,1)S(1)}, bf16[2,64,768]{2,1,0:T(8,128)(2,1)S(1)}, u32[]{:S(2)}, u32[]{:S(2)}) collective-permute-start(bf16[2,64,768]{2,1,0:T(8,128)(2,1)S(1)} %fusion.52), channel_id=1, source_target_pairs={{0,16},{4,20},{8,24},{12,28},{1,17},{5,21},{9,25},{13,29},{2,18},{... | collective-permute-start | bytes 589832 | tf_op jit(solution)/shard_map/ppermute | solution.py:183
  149.0 7.4 collective-permute-done.4
  156.5 9.3 %shard_map.340 = (f32[2,128,768]{2,1,0:T(8,128)S(1)}, f32[2,128,768]{2,1,0:T(8,128)S(1)}) custom-call(f32[2,128,768]{2,1,0:T(8,128)S(1)} %get-tuple-element.145.input_ref, f32[2,128,768]{2,1,0:T(8,128)S(1)} %get-tuple-element.149.query_ref, f32[2,64,768]{2,1,0:T(8,128)S(1)} %multiply_add_fusion.4.carried_ref, f32[64,768]{1,0:T(8,128)S(1)} %get-tuple-element.164.decay_ref, ...), custom_call_target="tpu_custom_call" | custom-call | bytes 2362368 | tf_op jit(solution)/shard_map/pallas_call | solution.py:154
  165.9 83.6 %all-gather.5.cloned.1.call-done = bf16[768,16384]{1,0:T(8,128)(2,1)} async-done(((bf16[24,16384]{1,0:T(8,128)(2,1)}), bf16[768,16384]{1,0:T(8,128)(2,1)}) %all-gather.5.cloned.1.call-update) | async-done | bytes 25165840 | tf_op jit(solution)/shard_map/all_gather | solution.py:577
  252.5 8.2 fusion.78
  260.7 9.7 %reshape.381 = bf16[32,24,4,768]{3,2,1,0:T(4,128)(2,1)} reshape(bf16[768,3072]{1,0:T(8,128)(2,1)} %get-tuple-element.148) | data formatting | bytes 9437184 | tf_op jit(solution)/shard_map/reshape | solution.py:543
  273.8 5.5 fusion.9
  292.3 35.3 %all_to_all.20 = bf16[8,128,640]{2,1,0:T(8,128)(2,1)} all-to-all(bf16[8,128,640]{2,1,0:T(8,128)(2,1)S(1)} %bitcast.144), channel_id=1, replica_groups=mesh['seq'=8,'batch'=4] {'seq'}, dimensions={0} | all-to-all | bytes 2621440 | tf_op jit(solution)/shard_map/all_to_all | solution.py:694
  327.6 10.9 %shard_map.341 = (bf16[1024,192]{1,0:T(8,128)(2,1)}, f32[1024,192]{1,0:T(8,128)}, f32[3,1024,128]{2,1,0:T(8,128)}) custom-call(bf16[1024,640]{1,0:T(8,128)(2,1)} %bitcast.140), custom_call_target="tpu_custom_call" | custom-call | tf_op jit(solution)/shard_map/pallas_call | solution.py:282
  346.2 9.7 %reshape.389 = bf16[32,24,4,768]{3,2,1,0:T(4,128)(2,1)} reshape(bf16[768,3072]{1,0:T(8,128)(2,1)} %get-tuple-element.147) | data formatting | bytes 9437184 | tf_op jit(solution)/shard_map/reshape | solution.py:543
  355.9 5.5 copy.120
  388.0 8.1 pad_maximum_fusion
  403.5 17.0 %all_to_all.21 = bf16[8,128,192]{1,2,0:T(8,128)(2,1)} all-to-all(bf16[8,128,192]{1,2,0:T(8,128)(2,1)S(1)} %bitcast.164), channel_id=1, replica_groups=mesh['seq'=8,'batch'=4] {'seq'}, dimensions={0} | all-to-all | bytes 786432 | tf_op jit(solution)/shard_map/all_to_all | solution.py:694
  422.5 12.6 %shard_map.342 = bf16[1024,640]{1,0:T(8,128)(2,1)} custom-call(bf16[1024,640]{1,0:T(8,128)(2,1)} %bitcast.141, bf16[1024,192]{1,0:T(8,128)(2,1)} %bitcast.160, f32[1024,192]{1,0:T(8,128)} %get-tuple-element.30.full_ref, f32[3,1024,128]{2,1,0:T(8,128)} %get-tuple-element.31.stat_ref), custom_call_target="tpu_custom_call" | custom-call | tf_op jit(solution)/shard_map/pallas_call | solution.py:299
  440.7 53.1 %all-to-all-done.3 = bf16[8,128,640]{2,1,0:T(8,128)(2,1)} async-done(((bf16[8,128,640]{2,1,0:T(8,128)(2,1)}), bf16[8,128,640]{2,1,0:T(8,128)(2,1)}, u32[]{:S(2)}, u32[]{:S(2)}) %all-to-all-start.3) | async-done | bytes 1310752 | tf_op jit(solution)/shard_map/all_to_all | solution.py:699
  531.2 6.4 copy-done
  545.7 9.3 %collective-permute-done.7 = bf16[2,64,768]{2,1,0:T(8,128)(2,1)S(1)} collective-permute-done((bf16[2,64,768]{2,1,0:T(8,128)(2,1)S(1)}, bf16[2,64,768]{2,1,0:T(8,128)(2,1)S(1)}, u32[]{:S(2)}, u32[]{:S(2)}) %collective-permute-start.7) | collective-permute-done | bytes 196640 | tf_op jit(solution)/shard_map/ppermute | solution.py:183
  558.2 8.6 %collective-permute-done.8 = bf16[2,64,768]{2,1,0:T(8,128)(2,1)S(1)} collective-permute-done((bf16[2,64,768]{2,1,0:T(8,128)(2,1)S(1)}, bf16[2,64,768]{2,1,0:T(8,128)(2,1)S(1)}, u32[]{:S(2)}, u32[]{:S(2)}) %collective-permute-start.8) | collective-permute-done | bytes 196640 | tf_op jit(solution)/shard_map/ppermute | solution.py:183
  566.9 20.8 %shard_map.344 = (f32[2,128,768]{2,1,0:T(8,128)S(1)}, f32[64,768]{1,0:T(8,128)S(1)}, f32[64,768]{1,0:T(8,128)S(1)}, f32[1,768]{1,0:T(1,128)S(1)}) custom-call(f32[2,128,768]{2,1,0:T(8,128)S(1)} %get-tuple-element.145.input_ref, f32[2,128,768]{2,1,0:T(8,128)S(1)} %get-tuple-element.154.input_ref.grad_ref, f32[2,64,768]{2,1,0:T(8,128)S(1)} %multiply_add_fusion.4.carried_ref, ...), custom_call_target="tpu_custom_call" | custom-call | bytes 2755584 | tf_op jit(solution)/shard_map/pallas_call | solution.py:154
  609.2 204.0 %reduce-scatter.3.cloned.1.call-done = bf16[24,12032]{1,0:T(8,128)(2,1)} async-done(((bf16[768,12032]{1,0:T(8,128)(2,1)}), bf16[24,12032]{1,0:T(8,128)(2,1)}) %reduce-scatter.3.cloned.1.call-update) | async-done | bytes 577552 | tf_op jit(solution)/shard_map/reduce_scatter | solution.py:582
  (344 shorter events, 188.1 us)
Async XLA Ops:
  7.2 70.8 %all-gather.3.cloned.1.call-start = ((), (), s32[]{:S(2)}) async-start(), calls=%async_computation.6 | async-start | bytes 4055040 | tf_op jit(solution)/shard_map/all_gather | solution.py:577
  14.3 235.2 %all-gather.5.cloned.1.call-start = ((), (), s32[]{:S(2)}) async-start(), calls=%async_computation.7 | async-start | bytes 25952256 | tf_op jit(solution)/shard_map/all_gather | solution.py:577
  83.2 4.8 collective-permute-start
  86.7 69.7 %copy-start.19 = (f32[64,768]{1,0:T(8,128)}, f32[64,768]{1,0:T(8,128)S(1)}, u32[]{:S(2)}) copy-start(f32[64,768]{1,0:T(8,128)S(1)} %get-tuple-element.163) | copy-start | bytes 589828
  93.2 7.6 collective-permute-start.1
  100.8 12.8 %collective-permute-start.2 = (bf16[2,64,768]{2,1,0:T(8,128)(2,1)S(1)}, bf16[2,64,768]{2,1,0:T(8,128)(2,1)S(1)}, u32[]{:S(2)}, u32[]{:S(2)}) collective-permute-start(bf16[2,64,768]{2,1,0:T(8,128)(2,1)S(1)} %collective-permute-done.1), channel_id=1, source_target_pairs={{0,4},{4,8},{8,12},{12,16},{16,20},{20,24},{24,28},{1,5},{5,9},{9,... | collective-permute-start | bytes 589832 | tf_op jit(solution)/shard_map/ppermute | solution.py:183
  113.6 15.3 %collective-permute-start.3 = (bf16[2,64,768]{2,1,0:T(8,128)(2,1)S(1)}, bf16[2,64,768]{2,1,0:T(8,128)(2,1)S(1)}, u32[]{:S(2)}, u32[]{:S(2)}) collective-permute-start(bf16[2,64,768]{2,1,0:T(8,128)(2,1)S(1)} %fusion.47), channel_id=1, source_target_pairs={{0,8},{4,12},{8,16},{12,20},{16,24},{20,28},{1,9},{5,13},{9,17},{1... | collective-permute-start | bytes 589832 | tf_op jit(solution)/shard_map/ppermute | solution.py:183
  129.0 27.4 %collective-permute-start.4 = (bf16[2,64,768]{2,1,0:T(8,128)(2,1)S(1)}, bf16[2,64,768]{2,1,0:T(8,128)(2,1)S(1)}, u32[]{:S(2)}, u32[]{:S(2)}) collective-permute-start(bf16[2,64,768]{2,1,0:T(8,128)(2,1)S(1)} %fusion.52), channel_id=1, source_target_pairs={{0,16},{4,20},{8,24},{12,28},{1,17},{5,21},{9,25},{13,29},{2,18},{... | collective-permute-start | bytes 589832 | tf_op jit(solution)/shard_map/ppermute | solution.py:183
  165.9 94.8 %copy-start.21 = (bf16[2,128,768]{2,1,0:T(8,128)(2,1)}, bf16[2,128,768]{2,1,0:T(8,128)(2,1)S(1)}, u32[]{:S(2)}) copy-start(bf16[2,128,768]{2,1,0:T(8,128)(2,1)S(1)} %convert_element_type.238) | copy-start | bytes 1179652
  251.3 22.4 %copy-start.55 = (f32[256]{0:T(256)}, f32[256]{0:T(256)S(1)}, u32[]{:S(2)}) copy-start(f32[256]{0:T(256)S(1)} %broadcast_multiply_fusion.6) | copy-start | bytes 3076
  281.4 81.4 %copy-start.5 = (f32[256,768]{1,0:T(8,128)}, f32[256,768]{1,0:T(8,128)S(1)}, u32[]{:S(2)}) copy-start(f32[256,768]{1,0:T(8,128)S(1)} %get-tuple-element.185) | copy-start | bytes 2359300
  340.5 20.9 %all-to-all-start.1 = ((bf16[8,128,192]{1,2,0:T(8,128)(2,1)}), bf16[8,128,192]{1,2,0:T(8,128)(2,1)}, u32[]{:S(2)}, u32[]{:S(2)}) async-start(bf16[8,128,192]{1,2,0:T(8,128)(2,1)} %copy.118), calls=%async_computation.1 | async-start | bytes 786432 | tf_op jit(solution)/shard_map/all_to_all | solution.py:699
  344.6 260.5 %reduce-scatter.5.cloned.1.call-start = ((), (), s32[]{:S(2)}) async-start(), calls=%async_computation.9 | async-start | bytes 10948608 | tf_op jit(solution)/shard_map/reduce_scatter | solution.py:582
  435.1 58.7 %all-to-all-start.3 = ((bf16[8,128,640]{2,1,0:T(8,128)(2,1)}), bf16[8,128,640]{2,1,0:T(8,128)(2,1)}, u32[]{:S(2)}, u32[]{:S(2)}) async-start(bf16[8,128,640]{2,1,0:T(8,128)(2,1)} %bitcast.146), calls=%async_computation.3 | async-start | bytes 2621440 | tf_op jit(solution)/shard_map/all_to_all | solution.py:699
  439.4 57.0 %copy-start.50 = (f32[768]{0:T(1024)S(1)}, f32[768]{0:T(1024)}, u32[]{:S(2)}) copy-start(f32[768]{0:T(1024)} %get-tuple-element.126) | copy-start | bytes 9220
  439.4 373.7 %reduce-scatter.3.cloned.1.call-start = ((), (), s32[]{:S(2)}) async-start(), calls=%async_computation.8 | async-start | bytes 19058688 | tf_op jit(solution)/shard_map/reduce_scatter | solution.py:582
  517.4 10.9 %collective-permute-start.5 = (bf16[2,64,768]{2,1,0:T(8,128)(2,1)S(1)}, bf16[2,64,768]{2,1,0:T(8,128)(2,1)S(1)}, u32[]{:S(2)}, u32[]{:S(2)}) collective-permute-start(bf16[2,64,768]{2,1,0:T(8,128)(2,1)S(1)} %convert_element_type.256), channel_id=1, source_target_pairs={{4,0},{8,4},{12,8},{16,12},{20,16},{24,20},{28,24},{5,1},{9,5},{13... | collective-permute-start | bytes 589832 | tf_op jit(solution)/shard_map/ppermute | solution.py:183
  528.3 12.7 %collective-permute-start.6 = (bf16[2,64,768]{2,1,0:T(8,128)(2,1)S(1)}, bf16[2,64,768]{2,1,0:T(8,128)(2,1)S(1)}, u32[]{:S(2)}, u32[]{:S(2)}) collective-permute-start(bf16[2,64,768]{2,1,0:T(8,128)(2,1)S(1)} %collective-permute-done.5), channel_id=1, source_target_pairs={{4,0},{8,4},{12,8},{16,12},{20,16},{24,20},{28,24},{5,1},{9,5},{13... | collective-permute-start | bytes 589832 | tf_op jit(solution)/shard_map/ppermute | solution.py:183
  541.0 14.0 %collective-permute-start.7 = (bf16[2,64,768]{2,1,0:T(8,128)(2,1)S(1)}, bf16[2,64,768]{2,1,0:T(8,128)(2,1)S(1)}, u32[]{:S(2)}, u32[]{:S(2)}) collective-permute-start(bf16[2,64,768]{2,1,0:T(8,128)(2,1)S(1)} %fusion.48), channel_id=1, source_target_pairs={{8,0},{12,4},{16,8},{20,12},{24,16},{28,20},{9,1},{13,5},{17,9},{2... | collective-permute-start | bytes 589832 | tf_op jit(solution)/shard_map/ppermute | solution.py:183
  555.2 32.6 %copy-start.4 = (f32[2,128,768]{2,1,0:T(8,128)S(1)}, f32[2,128,768]{2,1,0:T(8,128)}, u32[]{:S(2)}) copy-start(f32[2,128,768]{2,1,0:T(8,128)} %copy-done.3) | copy-start | bytes 2359300
  555.2 32.6 %copy-start.12 = (f32[2,128,768]{2,1,0:T(8,128)S(1)}, f32[2,128,768]{2,1,0:T(8,128)}, u32[]{:S(2)}) copy-start(f32[2,128,768]{2,1,0:T(8,128)} %get-tuple-element.146) | copy-start | bytes 2359300
  555.2 32.6 %copy-start.37 = (f32[2,3,768]{2,1,0:T(4,128)S(1)}, f32[2,3,768]{2,1,0:T(4,128)}, u32[]{:S(2)}) copy-start(f32[2,3,768]{2,1,0:T(4,128)} %copy-done.36) | copy-start | bytes 55300
  555.2 11.6 %collective-permute-start.8 = (bf16[2,64,768]{2,1,0:T(8,128)(2,1)S(1)}, bf16[2,64,768]{2,1,0:T(8,128)(2,1)S(1)}, u32[]{:S(2)}, u32[]{:S(2)}) collective-permute-start(bf16[2,64,768]{2,1,0:T(8,128)(2,1)S(1)} %fusion.53), channel_id=1, source_target_pairs={{16,0},{20,4},{24,8},{28,12},{17,1},{21,5},{25,9},{29,13},{18,2},{... | collective-permute-start | bytes 589832 | tf_op jit(solution)/shard_map/ppermute | solution.py:183
  588.8 6.0 collective-permute-start.9
  (72 other events, 337.1 us)
Sparse Core Ops, SparseCore 0:
  14.4 63.6 all-gather.2
  81.0 168.4 all-gather.4
  396.2 166.5 reduce-scatter.4
  605.2 207.8 reduce-scatter.2

commit v2 on v1

--- a/solution.py
+++ b/solution.py
@@ -183,15 +183,263 @@
     return lax.ppermute(block, axis, route)
 
 
-def carried_in(ends, block_power, direction):
+def carried_in(ends, decay, block_len, reverse):
+    seq_count, state_count, width = ends.shape
     count = lax.axis_size("seq")
-    carried = passed_along(ends.astype(bf16), "seq", direction).astype(f32)
-    distance = 1
-    while distance < count - 1:
-        arrived = passed_along(carried.astype(bf16), "seq", direction * distance).astype(f32)
-        carried = carried + jnp.power(block_power, distance)[None] * arrived
-        distance *= 2
-    return carried
+    part = state_count // count
+
+    def exchanged(parts):
+        return lax.all_to_all(parts.astype(bf16), "seq", split_axis=0, concat_axis=0, tiled=True)
+
+    parts = ends.reshape(seq_count, count, part, width).transpose(1, 0, 2, 3)
+    arrived = exchanged(parts.reshape(count, seq_count * part, width)).astype(f32)
+    rates = lax.dynamic_slice_in_dim(decay, lax.axis_index("seq") * part, part, 0)
+    power = jnp.tile(jnp.exp(-rates * block_len), (seq_count, 1))
+    state, joined = jnp.zeros_like(arrived[0]), [None] * count
+    for block in reversed(range(count)) if reverse else range(count):
+        joined[block] = state
+        state = power * state + arrived[block]
+    back = exchanged(jnp.stack(joined))
+    back = back.reshape(count, seq_count, part, width).transpose(1, 0, 2, 3)
+    return back.reshape(seq_count, state_count, width)
+
+
+MESH = pl.DeviceIdType.MESH
+box = (4, 2, 2, 2)
+
+
+def here():
+    seq, batch = lax.axis_index("seq"), lax.axis_index("batch")
+    return lax.div(seq, 2), lax.rem(seq, 2), lax.div(batch, 2), lax.rem(batch, 2)
+
+
+def device(z, x, y, core):
+    return (2 * z + x, 2 * y + core)
+
+
+def line_peer(z, step):
+    return lax.rem(z + step, box[0])
+
+
+def greet():
+    z, x, y, core = here()
+    barrier = pltpu.get_barrier_semaphore()
+    peers = [device(line_peer(z, step), x, y, core) for step in range(1, box[0])]
+    peers += [device(z, 1 - x, y, core), device(z, x, 1 - y, core), device(z, x, y, 1 - core)]
+    for peer in peers:
+        pl.semaphore_signal(barrier, inc=1, device_id=peer, device_id_type=MESH)
+    pl.semaphore_wait(barrier, len(peers))
+
+
+def staggered(count, stages, gap):
+    for turn in range(count + gap * (stages - 1)):
+        for stage in reversed(range(stages)):
+            chunk = turn - gap * stage
+            if 0 <= chunk < count:
+                yield stage, chunk
+
+
+def gather_kernel(plan, gap, *refs):
+    count = 1 + max(item[0] for item in plan)
+    ins, outs = refs[:count], refs[count : 2 * count]
+    send, receive, local = refs[2 * count :]
+    z, x, y, core = here()
+    greet()
+    started = {}
+
+    def push(chunk, slot, source, target, peer):
+        copy = pltpu.make_async_remote_copy(
+            src_ref=source,
+            dst_ref=target,
+            send_sem=send.at[chunk, slot],
+            recv_sem=receive.at[chunk, slot],
+            device_id=peer,
+            device_id_type=MESH,
+        )
+        copy.start()
+        started[chunk, slot] = copy
+
+    own = []
+    for chunk, (index, first, width, x_first) in enumerate(plan):
+        columns = pl.ds(first, width)
+        source = ins[index].at[:, columns]
+        target = outs[index].at[z, x, y, core, :, columns]
+        for step in range(1, box[0]):
+            push(chunk, step - 1, source, target, device(line_peer(z, step), x, y, core))
+        keep = pltpu.make_async_copy(source, target, local.at[chunk])
+        keep.start()
+        own.append(keep)
+
+    for stage, chunk in staggered(len(plan), 3, gap):
+        index, first, width, x_first = plan[chunk]
+        columns = pl.ds(first, width)
+        out = outs[index]
+        if stage == 0:
+            for step in range(1, box[0]):
+                started[chunk, step - 1].wait_recv()
+            own[chunk].wait()
+            part = out.at[:, x, y, core, :, columns]
+            peer = device(z, 1 - x, y, core) if x_first else device(z, x, 1 - y, core)
+            push(chunk, 3, part, part, peer)
+        elif stage == 1:
+            started[chunk, 3].wait_recv()
+            if x_first:
+                part, peer = out.at[:, :, y, core, :, columns], device(z, x, 1 - y, core)
+            else:
+                part, peer = out.at[:, x, :, core, :, columns], device(z, 1 - x, y, core)
+            push(chunk, 4, part, part, peer)
+        else:
+            started[chunk, 4].wait_recv()
+            part = out.at[:, :, :, core, :, columns]
+            push(chunk, 5, part, part, device(z, x, y, 1 - core))
+    for chunk in range(len(plan)):
+        started[chunk, 5].wait_recv()
+        for slot in range(6):
+            started[chunk, slot].wait_send()
+
+
+def gather_blocks(blocks, plan, gap=2, collective=0):
+    outs = [jax.ShapeDtypeStruct(box + b.shape, b.dtype) for b in blocks]
+    sent = sum(b.size * b.dtype.itemsize for b in blocks)
+    whole = pl.pallas_call(
+        functools.partial(gather_kernel, plan, gap),
+        out_shape=outs,
+        in_specs=[pl.BlockSpec(memory_space=pltpu.VMEM)] * len(blocks),
+        out_specs=[pl.BlockSpec(memory_space=pl.ANY)] * len(blocks),
+        scratch_shapes=[
+            pltpu.SemaphoreType.DMA((len(plan), 6)),
+            pltpu.SemaphoreType.DMA((len(plan), 6)),
+            pltpu.SemaphoreType.DMA((len(plan),)),
+        ],
+        cost_estimate=pl.CostEstimate(flops=0, bytes_accessed=64 * sent, transcendentals=0),
+        compiler_params=pltpu.CompilerParams(collective_id=collective, has_side_effects=True),
+    )(*blocks)
+    return [w.reshape((32 * w.shape[4], w.shape[5])) for w in whole]
+
+
+def add_into(total, other):
+    return (total.astype(f32) + other.astype(f32)).astype(bf16)
+
+
+def scatter_kernel(plan, gap, *refs):
+    count = 1 + max(item[0] for item in plan)
+    ins, outs = refs[:count], refs[count : 2 * count]
+    buffers = refs[2 * count : -3]
+    send, receive, local = refs[-3:]
+    z, x, y, core = here()
+    greet()
+    started = {}
+
+    def push(chunk, slot, source, target, peer):
+        copy = pltpu.make_async_remote_copy(
+            src_ref=source,
+            dst_ref=target,
+            send_sem=send.at[chunk, slot],
+            recv_sem=receive.at[chunk, slot],
+            device_id=peer,
+            device_id_type=MESH,
+        )
+        copy.start()
+        started[chunk, slot] = copy
+
+    loads = []
+    for chunk, (index, first, width, _) in enumerate(plan):
+        columns = pl.ds(first, width)
+        held, from_core = buffers[5 * chunk : 5 * chunk + 2]
+        grad = ins[index]
+        push(chunk, 0, grad.at[:, :, :, 1 - core, :, columns], from_core, device(z, x, y, 1 - core))
+        load = pltpu.make_async_copy(grad.at[:, :, :, core, :, columns], held, local.at[chunk])
+        load.start()
+        loads.append(load)
+
+    for stage, chunk in staggered(len(plan), 4, gap):
+        index, first, width, x_first = plan[chunk]
+        held, from_core, from_one, from_two, from_line = buffers[5 * chunk : 5 * chunk + 5]
+        to_x, to_y = device(z, 1 - x, y, core), device(z, x, 1 - y, core)
+        if stage == 0:
+            started[chunk, 0].wait_recv()
+            loads[chunk].wait()
+
+            @pl.loop(0, box[0])
+            def _(row):
+                for i in range(2):
+                    for j in range(2):
+                        held[row, i, j] = add_into(held[row, i, j], from_core[row, i, j])
+
+            if x_first:
+                push(chunk, 1, held.at[:, :, 1 - y], from_one, to_y)
+            else:
+                push(chunk, 1, held.at[:, 1 - x], from_one, to_x)
+        elif stage == 1:
+            started[chunk, 1].wait_recv()
+
+            @pl.loop(0, box[0])
+            def _(row):
+                for i in range(2):
+                    if x_first:
+                        held[row, i, y] = add_into(held[row, i, y], from_one[row, i])
+                    else:
+                        held[row, x, i] = add_into(held[row, x, i], from_one[row, i])
+
+            if x_first:
+                push(chunk, 2, held.at[:, 1 - x, y], from_two, to_x)
+            else:
+                push(chunk, 2, held.at[:, x, 1 - y], from_two, to_y)
+        elif stage == 2:
+            started[chunk, 2].wait_recv()
+
+            @pl.loop(0, box[0])
+            def _(row):
+                held[row, x, y] = add_into(held[row, x, y], from_two[row])
+
+            for step in range(1, box[0]):
+                peer = line_peer(z, step)
+                push(chunk, 2 + step, held.at[peer, x, y], from_line.at[step - 1], device(peer, x, y, core))
+        else:
+            total = held[z, x, y].astype(f32)
+            for step in range(1, box[0]):
+                started[chunk, 2 + step].wait_recv()
+                total = total + from_line[step - 1].astype(f32)
+            outs[index][:, pl.ds(first, width)] = total
+    for chunk in range(len(plan)):
+        for slot in range(6):
+            started[chunk, slot].wait_send()
+
+
+def scatter_blocks(grads, plan, gap=2, collective=1):
+    views = [g.reshape(box + (g.shape[0] // 32, g.shape[1])) for g in grads]
+    scratch = []
+    for index, _, width, _ in plan:
+        tile = (views[index].shape[4], width)
+        for lead in ((4, 2, 2), (4, 2, 2), (4, 2), (4,), (3,)):
+            scratch.append(pltpu.VMEM(lead + tile, bf16))
+    sent = sum(v.size * v.dtype.itemsize for v in views)
+    return pl.pallas_call(
+        functools.partial(scatter_kernel, plan, gap),
+        out_shape=[jax.ShapeDtypeStruct(v.shape[4:], f32) for v in views],
+        in_specs=[pl.BlockSpec(memory_space=pl.ANY)] * len(views),
+        out_specs=[pl.BlockSpec(memory_space=pltpu.VMEM)] * len(views),
+        scratch_shapes=scratch
+        + [
+            pltpu.SemaphoreType.DMA((len(plan), 6)),
+            pltpu.SemaphoreType.DMA((len(plan), 6)),
+            pltpu.SemaphoreType.DMA((len(plan),)),
+        ],
+        cost_estimate=pl.CostEstimate(flops=0, bytes_accessed=4 * sent, transcendentals=0),
+        compiler_params=pltpu.CompilerParams(
+            collective_id=collective, has_side_effects=True, vmem_limit_bytes=60 * 1024 * 1024
+        ),
+    )(*views)
+
+
+def chunked(widths, pieces):
+    plan = []
+    for index, (width, number) in enumerate(zip(widths, pieces)):
+        tiles = width // lanes
+        edges = [tiles * i // number for i in range(number + 1)]
+        for i in range(number):
+            plan.append((index, edges[i] * lanes, (edges[i + 1] - edges[i]) * lanes, len(plan) % 2 == 0))
+    return plan
 
 
 def split_heads(ref, scratch, heads, parts, first=0):
@@ -626,21 +874,24 @@
     small_count = small.shape[1]
     small_width = -(-small_count // lanes) * lanes
     small = jnp.pad(small, ((0, 0), (0, small_width - small_count)))
-    w_mixer_in, w_small = gathered([mixer_inputs, small])
     attend_cols = attend_inputs.shape[1]
-    w_mixer_out, w_up1, w_down1, w_attend_in, w_attend_out, w_up2, w_down2 = gathered(
-        [
-            mixer_output,
-            first_up,
-            fold_rows(first_down, share),
-            group_columns(attend_inputs, groups, padded),
-            attend_output,
-            second_up,
-            fold_rows(second_down, share),
-        ]
-    )
-    w_down1 = unfold_rows(w_down1, fold, share)
-    w_down2 = unfold_rows(w_down2, fold, share)
+    grouped = group_columns(attend_inputs, groups, padded)
+    by_kernel = seq_devices == 8 and lax.axis_size("batch") == 4
+    packed = [mixer_output, first_up, grouped, attend_output, second_up]
+    if by_kernel:
+        joint = jnp.concatenate([mixer_inputs, small], axis=1)
+        w_mixer_out, w_up1, w_attend_in, w_attend_out, w_up2 = gathered(packed)
+        widths = (joint.shape[1], model_width, model_width)
+        w_joint, w_down1, w_down2 = gather_blocks(
+            (joint, first_down, second_down), chunked(widths, (4, 6, 6)), gap=4
+        )
+        w_mixer_in, w_small = cut(w_joint, [mixer_inputs.shape[1], small_width])
+    else:
+        w_mixer_in, w_small = gathered([mixer_inputs, small])
+        packed += [fold_rows(first_down, share), fold_rows(second_down, share)]
+        w_mixer_out, w_up1, w_attend_in, w_attend_out, w_up2, w_down1, w_down2 = gathered(packed)
+        w_down1 = unfold_rows(w_down1, fold, share)
+        w_down2 = unfold_rows(w_down2, fold, share)
 
     rows = w_small.T.astype(f32)
     decay, table_in, table_out = rows[:states], rows[states : 2 * states], rows[2 * states : 3 * states]
@@ -668,9 +919,7 @@
     rim_rows = passed_along(keys_mixer[:, block_len - reach + 1 :], "seq", 1)
     extended = jnp.concatenate([rim_rows, keys_mixer], axis=1)
     inner, shift_back = jax.vjp(shift_mix, extended, taps, value_mixer)
-    block_power = jnp.exp(-decay * block_len)
-    ends = encode(inner, decay, False)
-    carried = carried_in(ends, block_power, 1)
+    carried = carried_in(encode(inner, decay, False), decay, block_len, False)
     wide = shaped(seq_count, block_len, model_width)
     state_y, gated = per_lane_tile(
         output_kernel,
@@ -743,7 +992,7 @@
     into_gated = into_gated.reshape(seq_count, block_len, model_width)
     query_mixer_grad = into_gated * state_y
     state_grad = into_gated * query_mixer
-    later = carried_in(encode(state_grad, decay, True), block_power, -1)
+    later = carried_in(encode(state_grad, decay, True), decay, block_len, True)
     table = shaped(states, model_width)
     inner_grad, weight_grad, power_grad, skip_grad = per_lane_tile(
         back_kernel,
@@ -774,22 +1023,20 @@
         axis=0,
     )
     small_grad = jnp.pad(small_rows, ((0, small_width - small_count), (0, 0))).T.astype(bf16)
-    attend_inputs_out, first_up_out, first_down_out, mixer_output_out, mixer_inputs_out, small_out = scattered(
-        [
-            attend_inputs_grad,
-            first_up_grad,
-            fold_all(first_down_grad, share, model_width),
-            mixer_output_grad,
-            mixer_inputs_grad,
-            small_grad,
-        ]
-    )
+    def unfolded(folded):
+        return folded.reshape(share, fold, model_width).transpose(1, 0, 2).reshape(share * fold, model_width)
+
+    last = [attend_inputs_grad, first_up_grad, mixer_output_grad, mixer_inputs_grad, small_grad]
+    if by_kernel:
+        last.append(first_down_grad)
+        plan = chunked([g.shape[1] for g in last], (4, 4, 2, 4, 2, 4))
+        *last, first_down_out = scatter_blocks(last, plan, gap=4)
+    else:
+        *last, folded = scattered(last + [fold_all(first_down_grad, share, model_width)])
+        first_down_out = unfolded(folded)
+    attend_inputs_out, first_up_out, mixer_output_out, mixer_inputs_out, small_out = last
     small_out = small_out.astype(f32)
     gains_at = 3 * states + reach
-
-    def unfolded(folded):
-        return folded.reshape(share, fold, model_width).transpose(1, 0, 2).reshape(share * fold, model_width)
-
     return (
         mixed,
         tokens_gradient,
@@ -803,7 +1050,7 @@
         mixer_output_out.astype(f32),
         small_out[:, gains_at + 1],
         first_up_out.astype(f32),
-        unfolded(first_down_out).astype(f32),
+        first_down_out.astype(f32),
         small_out[:, gains_at + 2],
         ungroup_columns(attend_inputs_out, groups, padded, attend_cols).astype(f32),
         attend_output_out.astype(f32),

time: 837 us -> 601 us (0.72)
  waiting for transfers between devices: 445 us -> 57.2 us
  Pallas kernels: 61.1 us -> 272 us
  local copies, waits for them, and re-layouts: 96.4 us -> 50.1 us
  starting transfers between devices: 60.5 us -> 35.1 us
  matrix products: 66.9 us -> 79.8 us
    pallas_call x0 -> x2, Pallas kernels: none -> 211 us  [the longest x1 111 us: gather_blocks(): pl.pallas_call(functools.partial(gather_kernel, plan, gap), out_shape=out...]
    reduce_scatter x2 -> x1, waiting for transfers between devices: 204 us -> 0.01 us  [scattered(): lax.psum_scatter(jnp.concatenate(parts, axis=1), everyone, scatter_dimens...]
    all_gather x2 -> x1, waiting for transfers between devices: 141 us -> 0.02 us  [gathered(): lax.all_gather(jnp.concatenate(parts, axis=1), everyone, axis=0, tiled=True)]
    ppermute x10 -> x2, starting transfers between devices: 51.8 us -> 4.23 us  [passed_along(): return lax.ppermute(block, axis, route)]
    ppermute x10 -> x2, waiting for transfers between devices: 47.3 us -> 5.79 us  [passed_along(): return lax.ppermute(block, axis, route)]
    all_to_all x2, waiting for transfers between devices: 53.1 us -> 30.8 us  [collect(): back = lax.all_to_all(parts, 'seq', split_axis=0, concat_axis=0, tiled=True)]
    all_to_all x0 -> x4, starting transfers between devices: none -> 20.6 us  [the longest x3 16.3 us: exchanged(): lax.all_to_all(parts.astype(bf16), 'seq', split_axis=0, concat_axis=0, ti...]
    all_to_all x0 -> x4, waiting for transfers between devices: none -> 20.5 us  [the longest x3 20.5 us: exchanged(): lax.all_to_all(parts.astype(bf16), 'seq', split_axis=0, concat_axis=0, ti...]
  transfers between devices with their start and end apart: 16 -> 10, of which waited for: 13 -> 6; matrix products, arithmetic and copies ran while one was open for 11% -> 17% of each run, Pallas kernels for 6% -> 42%
where the time goes in v2:
time: 601 us; the launch traced here: 590 us
  Pallas kernels  272 us (45%)
  matrix products  79.8 us (13%)
  waiting for transfers between devices  57.2 us (10%)
  local copies, waits for them, and re-layouts  50.1 us (8%)
  blocking collectives  46.6 us (8%)
  starting transfers between devices  35.1 us (6%)
  other arithmetic  33.3 us (6%)
  between operations  16 us (3%)
    pallas_call x1, Pallas kernels, gather_blocks(): pl.pallas_call(functools.partial(gather_kernel, plan, gap), out_shape=out...  111 us
    pallas_call x1, Pallas kernels, scatter_blocks(): pl.pallas_call(functools.partial(scatter_kernel, plan, gap), out_shape=[j...  100 us
    pallas_call x4, Pallas kernels, per_lane_tile(): pl.pallas_call(kernel, grid=(args[0].shape[-1] // lanes,), in_specs=[spec...  38 us
    all_to_all x1, blocking collectives, deal(): lax.all_to_all(parts, 'seq', split_axis=0, concat_axis=0, tiled=True)  34.7 us
    dot_general x8, matrix products, dense_back(): lax.dot_general(left, upstream, (((0,), (0,)), ((), ())), preferred_eleme...  31.4 us
    all_to_all x2, waiting for transfers between devices, collect(): back = lax.all_to_all(parts, 'seq', split_axis=0, concat_axis=0, tiled=True)  30.8 us
    dot_general x8, matrix products, dense_back(): lax.dot_general(upstream, weight, (((1,), (1,)), ((), ())), preferred_ele...  24.5 us
    dot_general x8, matrix products, dense(): return jnp.dot(left, weight, preferred_element_type=f32)  23.9 us
  transfers between devices with their start and end apart: 10, of which 6 were waited for; matrix products, arithmetic and copies ran while one was open for 17% of the time, Pallas kernels for 42%

profile of v2, /device:TPU:0, one launch (start us, length us, event | category | flops | bytes accessed | tf_op | source)
XLA Modules:
  0.0 590.0 jit_solution(12089160254808237982)
XLA Ops:
  14.6 110.6 %shard_map.339 = (bf16[4,2,2,2,24,2560]{5,4,3,2,1,0:T(8,128)(2,1)}, bf16[4,2,2,2,96,768]{5,4,3,2,1,0:T(8,128)(2,1)}, bf16[4,2,2,2,96,768]{5,4,3,2,1,0:T(8,128)(2,1)}) custom-call(bf16[24,2560]{1,0:T(8,128)(2,1)} %fusion.56.refs_0_, bf16[96,768]{1,0:T(8,128)(2,1)} %refs_1_.1, bf16[96,768]{1,0:T(8,128)(2,1)} %refs_2_.1), custom_call_target="tpu_custom_call" | custom-call | bytes 26738688 | tf_op jit(solution)/shard_map/pallas_call | solution.py:304
  141.8 6.1 %all-to-all-start = ((bf16[8,16,768]{2,1,0:T(8,128)(2,1)}), bf16[8,16,768]{2,1,0:T(8,128)(2,1)S(1)}, u32[]{:S(2)}, u32[]{:S(2)}) async-start(bf16[8,16,768]{2,1,0:T(8,128)(2,1)} %copy_bitcast_fusion.4), calls=%async_computation | async-start | bytes 393216 | tf_op jit(solution)/shard_map/all_to_all | solution.py:192
  147.9 12.1 %all-to-all-done = bf16[8,16,768]{2,1,0:T(8,128)(2,1)S(1)} async-done(((bf16[8,16,768]{2,1,0:T(8,128)(2,1)}), bf16[8,16,768]{2,1,0:T(8,128)(2,1)S(1)}, u32[]{:S(2)}, u32[]{:S(2)}) %all-to-all-start) | async-done | bytes 196640 | tf_op jit(solution)/shard_map/all_to_all | solution.py:192
  160.1 11.9 %all_to_all.40 = bf16[8,16,768]{2,1,0:T(8,128)(2,1)S(1)} all-to-all(bf16[8,16,768]{2,1,0:T(8,128)(2,1)S(1)} %constant_dynamic-update-slice_fusion), channel_id=1, replica_groups=mesh['seq'=8,'batch'=4] {'seq'}, dimensions={0} | all-to-all | bytes 393216 | tf_op jit(solution)/shard_map/all_to_all | solution.py:192
  172.1 9.3 %shard_map.341 = (f32[2,128,768]{2,1,0:T(8,128)S(1)}, f32[2,128,768]{2,1,0:T(8,128)S(1)}) custom-call(f32[2,128,768]{2,1,0:T(8,128)S(1)} %get-tuple-element.151.input_ref, f32[2,128,768]{2,1,0:T(8,128)S(1)} %get-tuple-element.153.query_ref, bf16[2,64,768]{2,1,0:T(8,128)(2,1)S(1)} %copy_bitcast_fusion.3.carried_ref, ...), custom_call_target="tpu_custom_call" | custom-call | bytes 2165760 | tf_op jit(solution)/shard_map/pallas_call | solution.py:154
  183.7 4.2 fusion.6
  190.3 4.4 convolution_convert_fusion.6
  199.9 34.7 %all_to_all.41 = bf16[8,128,640]{2,1,0:T(8,128)(2,1)} all-to-all(bf16[8,128,640]{2,1,0:T(8,128)(2,1)S(1)} %bitcast.249), channel_id=1, replica_groups=mesh['seq'=8,'batch'=4] {'seq'}, dimensions={0} | all-to-all | bytes 2621440 | tf_op jit(solution)/shard_map/all_to_all | solution.py:943
  234.5 10.9 %shard_map.342 = (bf16[1024,192]{1,0:T(8,128)(2,1)}, f32[1024,192]{1,0:T(8,128)}, f32[3,1024,128]{2,1,0:T(8,128)}) custom-call(bf16[1024,640]{1,0:T(8,128)(2,1)} %bitcast.245), custom_call_target="tpu_custom_call" | custom-call | tf_op jit(solution)/shard_map/pallas_call | solution.py:530
  251.6 10.8 %all-to-all-done.3 = bf16[8,128,192]{1,2,0:T(8,128)(2,1)} async-done(((bf16[8,128,192]{1,2,0:T(8,128)(2,1)}), bf16[8,128,192]{1,2,0:T(8,128)(2,1)}, u32[]{:S(2)}, u32[]{:S(2)}) %all-to-all-start.3) | async-done | bytes 393248 | tf_op jit(solution)/shard_map/all_to_all | solution.py:948
  290.9 4.3 all-to-all-start.4
  295.2 4.2 convolution_convert_fusion
  312.2 12.4 %shard_map.343 = bf16[1024,640]{1,0:T(8,128)(2,1)} custom-call(bf16[1024,640]{1,0:T(8,128)(2,1)} %bitcast.246, bf16[1024,192]{1,0:T(8,128)(2,1)} %bitcast.261, f32[1024,192]{1,0:T(8,128)} %get-tuple-element.42.full_ref, f32[3,1024,128]{2,1,0:T(8,128)} %get-tuple-element.43.stat_ref), custom_call_target="tpu_custom_call" | custom-call | tf_op jit(solution)/shard_map/pallas_call | solution.py:547
  324.6 6.0 %all-to-all-start.5 = ((bf16[8,128,640]{2,1,0:T(8,128)(2,1)}), bf16[8,128,640]{2,1,0:T(8,128)(2,1)}, u32[]{:S(2)}, u32[]{:S(2)}) async-start(bf16[8,128,640]{2,1,0:T(8,128)(2,1)} %bitcast.251), calls=%async_computation.5 | async-start | bytes 2621440 | tf_op jit(solution)/shard_map/all_to_all | solution.py:948
  330.8 9.3 %pad_maximum_fusion = bf16[768,6912]{1,0:T(8,128)(2,1)} fusion(bf16[768,768]{1,0:T(8,128)(2,1)} %convolution_convert_fusion.7, bf16[768,3072]{1,0:T(8,128)(2,1)} %bitcast.244, bf16[768,3072]{1,0:T(8,128)(2,1)} %convolution_convert_fusion.1), kind=kLoop, calls=%fused_computation | loop fusion | flops 31850496 | bytes 21233664 | tf_op jit(solution)/shard_map/concatenate | solution.py:831
  340.7 20.1 %all-to-all-done.5 = bf16[8,128,640]{2,1,0:T(8,128)(2,1)} async-done(((bf16[8,128,640]{2,1,0:T(8,128)(2,1)}), bf16[8,128,640]{2,1,0:T(8,128)(2,1)}, u32[]{:S(2)}, u32[]{:S(2)}) %all-to-all-start.5) | async-done | bytes 1310752 | tf_op jit(solution)/shard_map/all_to_all | solution.py:948
  363.4 4.2 multiply_reduce_fusion.1
  372.8 4.7 multiply_reduce_fusion.2
  394.1 6.6 %convolution_convert_fusion.2 = bf16[3072,768]{1,0:T(8,128)(2,1)} fusion(f32[256,768]{1,0:T(8,128)} %copy-done.21, f32[256,3072]{1,0:T(8,128)} %copy-done.64), kind=kOutput, calls=%fused_computation.3 | convolution fusion | flops 1217593344 | bytes 8650752 | tf_op jit(solution)/shard_map/dot_general | solution.py:742
  410.4 6.2 %all-to-all-start.7 = ((bf16[8,16,768]{2,1,0:T(8,128)(2,1)}), bf16[8,16,768]{2,1,0:T(8,128)(2,1)S(1)}, u32[]{:S(2)}, u32[]{:S(2)}) async-start(bf16[8,16,768]{2,1,0:T(8,128)(2,1)} %constant_dynamic-update-slice_fusion.13), calls=%async_computation.7 | async-start | bytes 393216 | tf_op jit(solution)/shard_map/all_to_all | solution.py:192
  416.6 4.7 convolution_convert_fusion.5
  421.3 8.4 %all-to-all-done.7 = bf16[8,16,768]{2,1,0:T(8,128)(2,1)S(1)} async-done(((bf16[8,16,768]{2,1,0:T(8,128)(2,1)}), bf16[8,16,768]{2,1,0:T(8,128)(2,1)S(1)}, u32[]{:S(2)}, u32[]{:S(2)}) %all-to-all-start.7) | async-done | bytes 196640 | tf_op jit(solution)/shard_map/all_to_all | solution.py:192
  429.7 21.2 %shard_map.345 = (f32[2,128,768]{2,1,0:T(8,128)S(1)}, f32[64,768]{1,0:T(8,128)S(1)}, f32[64,768]{1,0:T(8,128)S(1)}, f32[1,768]{1,0:T(1,128)S(1)}) custom-call(f32[2,128,768]{2,1,0:T(8,128)S(1)} %get-tuple-element.151.input_ref, f32[2,128,768]{2,1,0:T(8,128)S(1)} %get-tuple-element.158.input_ref.grad_ref, ...), custom_call_target="tpu_custom_call" | custom-call | bytes 2362368 | tf_op jit(solution)/shard_map/pallas_call | solution.py:154
  468.9 100.0 %shard_map.346 = (f32[24,2560]{1,0:T(8,128)}, f32[24,3072]{1,0:T(8,128)}, f32[24,768]{1,0:T(8,128)}, f32[24,2304]{1,0:T(8,128)}, f32[24,256]{1,0:T(8,128)}, /*index=5*/f32[96,768]{1,0:T(8,128)}) custom-call(bf16[4,2,2,2,24,2560]{5,4,3,2,1,0:T(8,128)(2,1)} %bitcast.241, bf16[4,2,2,2,24,3072]{5,4,3,2,1,0:T(8,128)(2,1)} %bitcast.242, ...), custom_call_target="tpu_custom_call" | custom-call | bytes 73924608 | tf_op jit(solution)/shard_map/pallas_call | solution.py:417
  (317 shorter events, 146.8 us)
Async XLA Ops:
  7.3 119.0 %copy-start.15 = (bf16[2,128,768]{2,1,0:T(8,128)(2,1)S(1)}, bf16[2,128,768]{2,1,0:T(8,128)(2,1)}, u32[]{:S(2)}) copy-start(bf16[2,128,768]{2,1,0:T(8,128)(2,1)} %param.20) | copy-start | bytes 1179652
  7.3 174.2 %all-gather.2.cloned.1.call-start = ((), (), s32[]{:S(2)}) async-start(), calls=%async_computation.9 | async-start | bytes 16220160 | tf_op jit(solution)/shard_map/all_gather | solution.py:825
  131.4 4.6 collective-permute-start
  141.8 18.2 %all-to-all-start = ((bf16[8,16,768]{2,1,0:T(8,128)(2,1)}), bf16[8,16,768]{2,1,0:T(8,128)(2,1)S(1)}, u32[]{:S(2)}, u32[]{:S(2)}) async-start(bf16[8,16,768]{2,1,0:T(8,128)(2,1)} %copy_bitcast_fusion.4), calls=%async_computation | async-start | bytes 393216 | tf_op jit(solution)/shard_map/all_to_all | solution.py:192
  190.1 178.2 %copy-start = (f32[256,768]{1,0:T(8,128)}, f32[256,768]{1,0:T(8,128)S(1)}, u32[]{:S(2)}) copy-start(f32[256,768]{1,0:T(8,128)S(1)} %get-tuple-element.184) | copy-start | bytes 2359300
  190.1 178.2 %copy-start.46 = (f32[256]{0:T(256)}, f32[256]{0:T(256)S(1)}, u32[]{:S(2)}) copy-start(f32[256]{0:T(256)S(1)} %broadcast_multiply_fusion.5) | copy-start | bytes 3076
  190.3 177.9 %copy-start.47 = (f32[256]{0:T(256)}, f32[256]{0:T(256)S(1)}, u32[]{:S(2)}) copy-start(f32[256]{0:T(256)S(1)} %fusion.77) | copy-start | bytes 3076
  199.8 51.7 %copy-start.58 = (s32[2]{0:T(128)S(1)}, s32[2]{0:T(128)}, u32[]{:S(2)}) copy-start(s32[2]{0:T(128)} %param.22) | copy-start | bytes 28
  247.4 15.0 %all-to-all-start.3 = ((bf16[8,128,192]{1,2,0:T(8,128)(2,1)}), bf16[8,128,192]{1,2,0:T(8,128)(2,1)}, u32[]{:S(2)}, u32[]{:S(2)}) async-start(bf16[8,128,192]{1,2,0:T(8,128)(2,1)} %copy.88), calls=%async_computation.3 | async-start | bytes 786432 | tf_op jit(solution)/shard_map/all_to_all | solution.py:948
  266.6 14.8 %copy-start.2 = (f32[256,768]{1,0:T(8,128)}, f32[256,768]{1,0:T(8,128)S(1)}, u32[]{:S(2)}) copy-start(f32[256,768]{1,0:T(8,128)S(1)} %get-tuple-element.186) | copy-start | bytes 2359300
  290.9 19.2 %all-to-all-start.4 = ((bf16[8,128,192]{1,2,0:T(8,128)(2,1)}), bf16[8,128,192]{1,2,0:T(8,128)(2,1)}, u32[]{:S(2)}, u32[]{:S(2)}) async-start(bf16[8,128,192]{1,2,0:T(8,128)(2,1)} %bitcast.264), calls=%async_computation.4 | async-start | bytes 786432 | tf_op jit(solution)/shard_map/all_to_all | solution.py:943
  324.6 36.2 %all-to-all-start.5 = ((bf16[8,128,640]{2,1,0:T(8,128)(2,1)}), bf16[8,128,640]{2,1,0:T(8,128)(2,1)}, u32[]{:S(2)}, u32[]{:S(2)}) async-start(bf16[8,128,640]{2,1,0:T(8,128)(2,1)} %bitcast.251), calls=%async_computation.5 | async-start | bytes 2621440 | tf_op jit(solution)/shard_map/all_to_all | solution.py:948
  330.5 245.4 %reduce-scatter.2.cloned.1.call-start = ((), (), s32[]{:S(2)}) async-start(), calls=%async_computation.10 | async-start | bytes 10948608 | tf_op jit(solution)/shard_map/reduce_scatter | solution.py:830
  369.8 8.7 %copy-start.21 = (f32[256,768]{1,0:T(8,128)}, f32[256,768]{1,0:T(8,128)S(1)}, u32[]{:S(2)}) copy-start(f32[256,768]{1,0:T(8,128)S(1)} %add_add_fusion.5) | copy-start | bytes 2359300
  387.3 17.2 %all-to-all-start.6 = ((bf16[8,16,768]{2,1,0:T(8,128)(2,1)}), bf16[8,16,768]{2,1,0:T(8,128)(2,1)}, u32[]{:S(2)}, u32[]{:S(2)}) async-start(bf16[8,16,768]{2,1,0:T(8,128)(2,1)} %copy_bitcast_fusion.1), calls=%async_computation.6 | async-start | bytes 393216 | tf_op jit(solution)/shard_map/all_to_all | solution.py:192
  400.7 15.8 %copy-start.1 = (f32[256,768]{1,0:T(8,128)S(1)}, f32[256,768]{1,0:T(8,128)}, u32[]{:S(2)}) copy-start(f32[256,768]{1,0:T(8,128)} %copy-done) | copy-start | bytes 2359300
  410.4 19.3 %all-to-all-start.7 = ((bf16[8,16,768]{2,1,0:T(8,128)(2,1)}), bf16[8,16,768]{2,1,0:T(8,128)(2,1)S(1)}, u32[]{:S(2)}, u32[]{:S(2)}) async-start(bf16[8,16,768]{2,1,0:T(8,128)(2,1)} %constant_dynamic-update-slice_fusion.13), calls=%async_computation.7 | async-start | bytes 393216 | tf_op jit(solution)/shard_map/all_to_all | solution.py:192
  429.7 21.3 %copy-start.10 = (f32[2,128,2304]{2,1,0:T(8,128)S(1)}, f32[2,128,2304]{2,1,0:T(8,128)}, u32[]{:S(2)}) copy-start(f32[2,128,2304]{2,1,0:T(8,128)} %copy-done.9) | copy-start | bytes 7077892
  453.9 6.9 %copy-start.29 = (bf16[2,128,768]{2,1,0:T(8,128)(2,1)S(1)}, bf16[2,128,768]{2,1,0:T(8,128)(2,1)}, u32[]{:S(2)}) copy-start(bf16[2,128,768]{2,1,0:T(8,128)(2,1)} %get-tuple-element.157) | copy-start | bytes 1179652
  453.9 6.0 %collective-permute-start.1 = (f32[2,3,768]{2,1,0:T(4,128)S(1)}, f32[2,3,768]{2,1,0:T(4,128)S(1)}, u32[]{:S(2)}, u32[]{:S(2)}) collective-permute-start(f32[2,3,768]{2,1,0:T(4,128)S(1)} %pad_add_fusion.1), channel_id=1, source_target_pairs={{4,0},{8,4},{12,8},{16,12},{20,16},{24,20},{28,24},{5,1},{9,5},{13... | collective-permute-start | bytes 55304 | tf_op jit(solution)/shard_map/ppermute | solution.py:183
  568.9 11.1 %copy-start.35 = (f32[24,2304]{1,0:T(8,128)S(1)}, f32[24,2304]{1,0:T(8,128)}, u32[]{:S(2)}) copy-start(f32[24,2304]{1,0:T(8,128)} %get-tuple-element.214) | copy-start | bytes 663556
  568.9 11.8 %copy-start.38 = (f32[24,768]{1,0:T(8,128)S(1)}, f32[24,768]{1,0:T(8,128)}, u32[]{:S(2)}) copy-start(f32[24,768]{1,0:T(8,128)} %get-tuple-element.220) | copy-start | bytes 221188
  568.9 12.4 %copy-start.34 = (f32[24,3072]{1,0:T(8,128)S(1)}, f32[24,3072]{1,0:T(8,128)}, u32[]{:S(2)}) copy-start(f32[24,3072]{1,0:T(8,128)} %get-tuple-element.222) | copy-start | bytes 884740
  570.4 11.6 %copy-start.33 = (f32[96,768]{1,0:T(8,128)S(1)}, f32[96,768]{1,0:T(8,128)}, u32[]{:S(2)}) copy-start(f32[96,768]{1,0:T(8,128)} %get-tuple-element.223) | copy-start | bytes 884740
  (59 other events, 237.6 us)
Sparse Core Ops, SparseCore 0:
  13.3 148.7 all-gather.1
  340.2 152.5 reduce-scatter.1

commit v3 on v2

--- a/solution.py
+++ b/solution.py
@@ -321,10 +321,10 @@
     return (total.astype(f32) + other.astype(f32)).astype(bf16)
 
 
-def scatter_kernel(plan, gap, *refs):
-    count = 1 + max(item[0] for item in plan)
-    ins, outs = refs[:count], refs[count : 2 * count]
-    buffers = refs[2 * count : -3]
+def scatter_kernel(plan, gap, finish, counts, *refs):
+    count, out_count = counts
+    ins, results = refs[:count], refs[count : count + out_count]
+    outs, buffers = refs[count + out_count : 2 * count + out_count], refs[2 * count + out_count : -3]
     send, receive, local = refs[-3:]
     z, x, y, core = here()
     greet()
@@ -401,24 +401,26 @@
                 started[chunk, 2 + step].wait_recv()
                 total = total + from_line[step - 1].astype(f32)
             outs[index][:, pl.ds(first, width)] = total
+            if not any(item[0] == index for item in plan[chunk + 1 :]):
+                finish(index, outs[index], results)
     for chunk in range(len(plan)):
         for slot in range(6):
             started[chunk, slot].wait_send()
 
 
-def scatter_blocks(grads, plan, gap=2, collective=1):
+def scatter_blocks(grads, plan, finish, results, gap=2, collective=1):
     views = [g.reshape(box + (g.shape[0] // 32, g.shape[1])) for g in grads]
-    scratch = []
+    scratch = [pltpu.VMEM(v.shape[4:], f32) for v in views]
     for index, _, width, _ in plan:
         tile = (views[index].shape[4], width)
         for lead in ((4, 2, 2), (4, 2, 2), (4, 2), (4,), (3,)):
             scratch.append(pltpu.VMEM(lead + tile, bf16))
     sent = sum(v.size * v.dtype.itemsize for v in views)
     return pl.pallas_call(
-        functools.partial(scatter_kernel, plan, gap),
-        out_shape=[jax.ShapeDtypeStruct(v.shape[4:], f32) for v in views],
+        functools.partial(scatter_kernel, plan, gap, finish, (len(views), len(results))),
+        out_shape=list(results),
         in_specs=[pl.BlockSpec(memory_space=pl.ANY)] * len(views),
-        out_specs=[pl.BlockSpec(memory_space=pltpu.VMEM)] * len(views),
+        out_specs=[pl.BlockSpec(memory_space=pltpu.VMEM)] * len(results),
         scratch_shapes=scratch
         + [
             pltpu.SemaphoreType.DMA((len(plan), 6)),
@@ -477,6 +479,8 @@
             )
             stat_ref[head, first:extent, :] = jnp.broadcast_to(top + jnp.log(whole), (block, lanes))
 
+    if low_ref.shape[1] > heads * HEAD_DIM:
+        low_ref[:, heads * HEAD_DIM :] = jnp.zeros((length, low_ref.shape[1] - heads * HEAD_DIM), bf16)
     for head in range(heads):
         place = slice(head * HEAD_DIM, (head + 1) * HEAD_DIM)
         full_ref[:, place] = outs[head]
@@ -530,7 +534,7 @@
     return pl.pallas_call(
         functools.partial(attend_kernel, heads, block, HEAD_DIM ** (-0.5)),
         out_shape=[
-            shaped(length, width, dtype=bf16),
+            shaped(length, -(-width // lanes) * lanes, dtype=bf16),
             shaped(length, width),
             shaped(heads, length, lanes),
         ],
@@ -806,6 +810,13 @@
     return jnp.pad(grouped, ((0, 0), (0, 0), (0, padded - 3 * part))).reshape(rows, groups * padded)
 
 
+def pad_groups(weight, groups, padded):
+    rows, columns = weight.shape
+    part = rows // groups
+    grouped = weight.reshape(groups, part, columns)
+    return jnp.pad(grouped, ((0, 0), (0, padded - part), (0, 0))).reshape(groups * padded, columns)
+
+
 def ungroup_columns(grouped, groups, padded, columns):
     rows = grouped.shape[0]
     part = columns // 3 // groups
@@ -819,6 +830,11 @@
         pieces.append(array[:, start : start + width])
         start += width
     return pieces
+
+
+def cut_last(array, count):
+    width = array.shape[-1] // count
+    return [array[..., i * width : (i + 1) * width] for i in range(count)]
 
 
 def gathered(parts):
@@ -867,6 +883,7 @@
     groups = HEADS // heads
     group_width = heads * HEAD_DIM
     padded = -(-3 * group_width // lanes) * lanes if dealt else 3 * group_width
+    out_width = -(-group_width // lanes) * lanes if dealt else group_width
 
     columns = [decay_rate, state_in, state_out, shift_taps]
     columns += [g[:, None] for g in (mixer_gain, first_gain, attend_gain, second_gain, state_skip)]
@@ -881,11 +898,11 @@
     if by_kernel:
         joint = jnp.concatenate([mixer_inputs, small], axis=1)
         w_mixer_out, w_up1, w_attend_in, w_attend_out, w_up2 = gathered(packed)
-        widths = (joint.shape[1], model_width, model_width)
-        w_joint, w_down1, w_down2 = gather_blocks(
-            (joint, first_down, second_down), chunked(widths, (4, 6, 6)), gap=4
-        )
+        widths = (joint.shape[1], model_width)
+        w_joint, w_down1 = gather_blocks((joint, first_down), chunked(widths, (4, 6)), gap=3)
         w_mixer_in, w_small = cut(w_joint, [mixer_inputs.shape[1], small_width])
+        second_down, w_small = lax.optimization_barrier((second_down, w_small))
+        w_down2 = lax.all_gather(second_down, everyone, axis=0, tiled=True)
     else:
         w_mixer_in, w_small = gathered([mixer_inputs, small])
         packed += [fold_rows(first_down, share), fold_rows(second_down, share)]
@@ -938,7 +955,8 @@
         block = min(256, length)
 
         def deal(array, width):
-            parts = array.reshape(seq_count, block_len, groups, width).transpose(0, 2, 1, 3)
+            array = array.reshape(seq_count, block_len, groups * width)
+            parts = jnp.stack(cut_last(array, groups), axis=1)
             parts = parts.reshape(seq_count * groups, block_len, width)
             dealt_parts = lax.all_to_all(parts, "seq", split_axis=0, concat_axis=0, tiled=True)
             return dealt_parts.reshape(length, width)
@@ -946,12 +964,14 @@
         def collect(array, width):
             parts = array.reshape(seq_devices, block_len, width)
             back = lax.all_to_all(parts, "seq", split_axis=0, concat_axis=0, tiled=True)
-            back = back.reshape(seq_count, groups, block_len, width).transpose(0, 2, 1, 3)
+            back = back.reshape(seq_count, groups, block_len, width)
+            back = jnp.concatenate([back[:, group] for group in range(groups)], axis=-1)
             return back.reshape(row_count, groups * width)
 
         qkv = deal(proj_low, padded)
         attended_part, attended_full, stat = attend_whole(qkv, heads, block)
-        attended_low = collect(attended_part, group_width)
+        attended_low = collect(attended_part, out_width)
+        w_attend_out = pad_groups(w_attend_out, groups, out_width)
     else:
         attended, attended_back = general_attention(
             proj_low, seq_count, block_len, places, any_live, longest
@@ -968,12 +988,15 @@
     into_attended, attend_output_grad = dense_back(
         attended_low, w_attend_out, upstream.astype(bf16)
     )
-    second_up_out, second_down_out, attend_output_out = scattered(
-        [second_up_grad, fold_all(second_down_grad, share, model_width), attend_output_grad]
-    )
+    if dealt:
+        attend_output_grad = attend_output_grad.reshape(groups, out_width, model_width)
+        attend_output_grad = attend_output_grad[:, :group_width].reshape(model_width, model_width)
+    early = [second_up_grad, fold_all(second_down_grad, share, model_width), attend_output_grad]
+    early_widths = [g.shape[1] for g in early]
+    early = jnp.concatenate(early, axis=1)
     dout_low = into_attended.astype(bf16)
     if dealt:
-        dout = deal(dout_low, group_width)
+        dout, early = lax.optimization_barrier((deal(dout_low, out_width), early))
         proj_grad = collect(
             attend_whole_back(qkv, dout, attended_full, stat, heads, block), padded
         )
@@ -982,6 +1005,8 @@
         proj_grad = jnp.concatenate(
             [p.reshape(row_count, model_width) for p in parts], axis=1
         ).astype(bf16)
+    early = lax.psum_scatter(early, everyone, scatter_dimension=0, tiled=True)
+    second_up_out, second_down_out, attend_output_out = cut(early, early_widths)
     into_normed, attend_inputs_grad = dense_back(normed_low_attend, w_attend_in, proj_grad)
     into_resid, attend_gain_grad = back_attend(into_normed)
     upstream = upstream + into_resid
@@ -1026,35 +1051,65 @@
     def unfolded(folded):
         return folded.reshape(share, fold, model_width).transpose(1, 0, 2).reshape(share * fold, model_width)
 
+    gains_at = 3 * states + reach
+    table_edges = [0, states, 2 * states, 3 * states, gains_at, small_width]
+
+    def tables_of(block):
+        return [block[:, a:b] for a, b in zip(table_edges, table_edges[1:])]
+
     last = [attend_inputs_grad, first_up_grad, mixer_output_grad, mixer_inputs_grad, small_grad]
     if by_kernel:
         last.append(first_down_grad)
         plan = chunked([g.shape[1] for g in last], (4, 4, 2, 4, 2, 4))
-        *last, first_down_out = scatter_blocks(last, plan, gap=4)
+        part = attend_cols // 3 // groups
+
+        def finish(index, block, results):
+            if index == 0:
+                for group in range(groups):
+                    for kind in range(3):
+                        start = (kind * groups + group) * part
+                        source = group * padded + kind * part
+                        results[0][:, start : start + part] = block[:, source : source + part]
+            elif index == 4:
+                for place, table in enumerate(tables_of(block)):
+                    results[5 + place][...] = table
+            else:
+                results[{1: 1, 2: 2, 3: 3, 5: 4}[index]][...] = block[...]
+
+        widths = [attend_cols] + [g.shape[1] for g in last[1:4]]
+        results = [shaped(share, w) for w in widths] + [shaped(share * fold, model_width)]
+        results += [shaped(share, b - a) for a, b in zip(table_edges, table_edges[1:])]
+        attend_inputs_out, first_up_out, mixer_output_out, mixer_inputs_out, first_down_out, *tables = (
+            scatter_blocks(last, plan, finish, results, gap=4)
+        )
     else:
         *last, folded = scattered(last + [fold_all(first_down_grad, share, model_width)])
-        first_down_out = unfolded(folded)
-    attend_inputs_out, first_up_out, mixer_output_out, mixer_inputs_out, small_out = last
-    small_out = small_out.astype(f32)
-    gains_at = 3 * states + reach
+        first_down_out = unfolded(folded).astype(f32)
+        grouped, first_up_out, mixer_output_out, mixer_inputs_out, small_out = (
+            g.astype(f32) for g in last
+        )
+        attend_inputs_out = ungroup_columns(grouped, groups, padded, attend_cols)
+        tables = tables_of(small_out)
+    decay_out, in_out, out_out, taps_out, vectors = tables
+
     return (
         mixed,
         tokens_gradient,
-        small_out[:, gains_at],
-        mixer_inputs_out.astype(f32),
-        small_out[:, 3 * states : gains_at],
-        small_out[:, :states],
-        small_out[:, states : 2 * states],
-        small_out[:, 2 * states : 3 * states],
-        small_out[:, gains_at + 4],
-        mixer_output_out.astype(f32),
-        small_out[:, gains_at + 1],
-        first_up_out.astype(f32),
-        first_down_out.astype(f32),
-        small_out[:, gains_at + 2],
-        ungroup_columns(attend_inputs_out, groups, padded, attend_cols).astype(f32),
+        vectors[:, 0],
+        mixer_inputs_out,
+        taps_out,
+        decay_out,
+        in_out,
+        out_out,
+        vectors[:, 4],
+        mixer_output_out,
+        vectors[:, 1],
+        first_up_out,
+        first_down_out,
+        vectors[:, 2],
+        attend_inputs_out,
         attend_output_out.astype(f32),
-        small_out[:, gains_at + 3],
+        vectors[:, 3],
         second_up_out.astype(f32),
         unfolded(second_down_out).astype(f32),
     )

time: 601 us -> 601 us (level); the launches traced: 590 us -> 599 us
  Pallas kernels: 272 us -> 237 us
  blocking collectives: 46.6 us -> 80.1 us
  waiting for transfers between devices: 57.2 us -> 69 us
    pallas_call x1, Pallas kernels: 111 us -> 75.8 us  [gather_blocks(): pl.pallas_call(functools.partial(gather_kernel, plan, gap), out_shape=out...]
    all_to_all x1, blocking collectives: 34.7 us -> 63.2 us  [deal(): lax.all_to_all(parts, 'seq', split_axis=0, concat_axis=0, tiled=True)]
    unnamed x163 -> x188, local copies, waits for them, and re-layouts: 14.5 us -> 25 us
    all_to_all x2, waiting for transfers between devices: 30.8 us -> 40.9 us  [collect(): back = lax.all_to_all(parts, 'seq', split_axis=0, concat_axis=0, tiled=True)]
    reshape x6 -> x0, local copies, waits for them, and re-layouts: 9.53 us -> none  [the longest x2 5.42 us: deal(): array.reshape(seq_count, block_len, groups, width).transpose(0, 2, 1, 3)]
    transpose x5 -> x0, local copies, waits for them, and re-layouts: 7.29 us -> none  [the longest x2 3.81 us: collect(): back.reshape(seq_count, groups, block_len, width).transpose(0, 2, 1, 3)]
    dot_general x8, matrix products: 23.9 us -> 30.2 us  [dense(): return jnp.dot(left, weight, preferred_element_type=f32)]
  transfers between devices with their start and end apart: 10 -> 11, of which waited for: 6 -> 8; matrix products, arithmetic and copies ran while one was open for 17% -> 19% of each run, Pallas kernels for 42% -> 37%
where the time goes in v3:
time: 601 us; the launch traced here: 599 us
  Pallas kernels  237 us (39%)
  matrix products  82.9 us (14%)
  blocking collectives  80.1 us (13%)
  waiting for transfers between devices  69 us (11%)
  local copies, waits for them, and re-layouts  48.3 us (8%)
  starting transfers between devices  33.3 us (6%)
  other arithmetic  32.8 us (5%)
  between operations  15.6 us (3%)
    pallas_call x1, Pallas kernels, scatter_blocks(): pl.pallas_call(functools.partial(scatter_kernel, plan, gap, finish, (len(...  99.8 us
    pallas_call x1, Pallas kernels, gather_blocks(): pl.pallas_call(functools.partial(gather_kernel, plan, gap), out_shape=out...  75.8 us
    all_to_all x1, blocking collectives, deal(): lax.all_to_all(parts, 'seq', split_axis=0, concat_axis=0, tiled=True)  63.2 us
    all_to_all x2, waiting for transfers between devices, collect(): back = lax.all_to_all(parts, 'seq', split_axis=0, concat_axis=0, tiled=True)  40.9 us
    pallas_call x4, Pallas kernels, per_lane_tile(): pl.pallas_call(kernel, grid=(args[0].shape[-1] // lanes,), in_specs=[spec...  38 us
    dot_general x8, matrix products, dense_back(): lax.dot_general(left, upstream, (((0,), (0,)), ((), ())), preferred_eleme...  32.6 us
    dot_general x8, matrix products, dense(): return jnp.dot(left, weight, preferred_element_type=f32)  30.2 us
    unnamed x188, local copies, waits for them, and re-layouts  25 us
  transfers between devices with their start and end apart: 11, of which 8 were waited for; matrix products, arithmetic and copies ran while one was open for 19% of the time, Pallas kernels for 37%

profile of v3, /device:TPU:0, one launch (start us, length us, event | category | flops | bytes accessed | tf_op | source)
XLA Modules:
  0.0 599.1 jit_solution(14252377473084384211)
XLA Ops:
  14.6 75.8 %shard_map.339 = (bf16[4,2,2,2,24,2560]{5,4,3,2,1,0:T(8,128)(2,1)}, bf16[4,2,2,2,96,768]{5,4,3,2,1,0:T(8,128)(2,1)}) custom-call(bf16[24,2560]{1,0:T(8,128)(2,1)} %fusion.49.refs_0_, bf16[96,768]{1,0:T(8,128)(2,1)} %refs_1_.1), custom_call_target="tpu_custom_call" | custom-call | bytes 17301504 | tf_op jit(solution)/shard_map/pallas_call | solution.py:304
  105.8 7.0 %all-to-all-start = ((bf16[8,16,768]{2,1,0:T(8,128)(2,1)}), bf16[8,16,768]{2,1,0:T(8,128)(2,1)S(1)}, u32[]{:S(2)}, u32[]{:S(2)}) async-start(bf16[8,16,768]{2,1,0:T(8,128)(2,1)} %copy_bitcast_fusion.4), calls=%async_computation | async-start | bytes 393216 | tf_op jit(solution)/shard_map/all_to_all | solution.py:192
  113.6 12.4 %all-to-all-done = bf16[8,16,768]{2,1,0:T(8,128)(2,1)S(1)} async-done(((bf16[8,16,768]{2,1,0:T(8,128)(2,1)}), bf16[8,16,768]{2,1,0:T(8,128)(2,1)S(1)}, u32[]{:S(2)}, u32[]{:S(2)}) %all-to-all-start) | async-done | bytes 196640 | tf_op jit(solution)/shard_map/all_to_all | solution.py:192
  126.2 16.9 %all_to_all.40 = bf16[8,16,768]{2,1,0:T(8,128)(2,1)S(1)} all-to-all(bf16[8,16,768]{2,1,0:T(8,128)(2,1)S(1)} %constant_dynamic-update-slice_fusion), channel_id=1, replica_groups=mesh['seq'=8,'batch'=4] {'seq'}, dimensions={0} | all-to-all | bytes 393216 | tf_op jit(solution)/shard_map/all_to_all | solution.py:192
  143.1 9.3 %shard_map.341 = (f32[2,128,768]{2,1,0:T(8,128)S(1)}, f32[2,128,768]{2,1,0:T(8,128)S(1)}) custom-call(f32[2,128,768]{2,1,0:T(8,128)S(1)} %get-tuple-element.165.input_ref, f32[2,128,768]{2,1,0:T(8,128)S(1)} %get-tuple-element.167.query_ref, bf16[2,64,768]{2,1,0:T(8,128)(2,1)S(1)} %copy_bitcast_fusion.3.carried_ref, ...), custom_call_target="tpu_custom_call" | custom-call | bytes 2165760 | tf_op jit(solution)/shard_map/pallas_call | solution.py:154
  153.2 4.6 all-gather.3.cloned.1.call-done
  164.0 6.3 %fusion.91 = (f32[256]{0:T(256)S(1)}, f32[256,768]{1,0:T(8,128)S(1)}) fusion(f32[256,768]{1,0:T(8,128)S(1)} %get-tuple-element.208, bf16[3072,768]{1,0:T(8,128)(2,1)} %bitcast.312, f32[256,3072]{1,0:T(8,128)S(1)} %fusion.6), kind=kOutput, calls=%fused_computation.258 | convolution fusion | flops 1215430400 | bytes 9438208 | tf_op jit(solution)/shard_map/dot_general | solution.py:739
  172.4 63.2 %all_to_all.41 = bf16[8,128,640]{2,1,0:T(8,128)(2,1)} all-to-all(bf16[8,128,640]{2,1,0:T(8,128)(2,1)S(1)} %bitcast.253), channel_id=1, replica_groups=mesh['seq'=8,'batch'=4] {'seq'}, dimensions={0} | all-to-all | bytes 2621440 | tf_op jit(solution)/shard_map/all_to_all | solution.py:961
  235.6 10.9 %shard_map.342 = (bf16[1024,256]{1,0:T(8,128)(2,1)}, f32[1024,192]{1,0:T(8,128)}, f32[3,1024,128]{2,1,0:T(8,128)}) custom-call(bf16[1024,640]{1,0:T(8,128)(2,1)} %bitcast.248), custom_call_target="tpu_custom_call" | custom-call | tf_op jit(solution)/shard_map/pallas_call | solution.py:534
  253.3 11.6 %all-to-all-done.3 = bf16[8,128,256]{2,1,0:T(8,128)(2,1)} async-done(((bf16[8,128,256]{2,1,0:T(8,128)(2,1)}), bf16[8,128,256]{2,1,0:T(8,128)(2,1)}, u32[]{:S(2)}, u32[]{:S(2)}) %all-to-all-start.3) | async-done | bytes 524320 | tf_op jit(solution)/shard_map/all_to_all | solution.py:966
  269.9 5.5 fusion.2
  275.4 5.5 convolution_add_fusion.2
  302.4 4.4 all-to-all-start.4
  308.2 4.7 copy.85
  315.1 8.1 %pad_maximum_fusion = bf16[768,6912]{1,0:T(8,128)(2,1)} fusion(bf16[768,768]{1,0:T(8,128)(2,1)S(1)} %bitcast.263, bf16[768,3072]{1,0:T(8,128)(2,1)S(1)} %bitcast.247, bf16[768,3072]{1,0:T(8,128)(2,1)S(1)} %bitcast.245), kind=kLoop, calls=%fused_computation | loop fusion | flops 31850496 | bytes 21233664 | tf_op jit(solution)/shard_map/concatenate | solution.py:996
  323.2 12.5 %shard_map.343 = bf16[1024,640]{1,0:T(8,128)(2,1)} custom-call(bf16[1024,640]{1,0:T(8,128)(2,1)} %bitcast.249, bf16[1024,256]{1,0:T(8,128)(2,1)} %bitcast.43.dout_ref, f32[1024,192]{1,0:T(8,128)} %get-tuple-element.51.full_ref, f32[3,1024,128]{2,1,0:T(8,128)} %get-tuple-element.52.stat_ref), custom_call_target="tpu_custom_call" | custom-call | tf_op jit(solution)/shard_map/pallas_call | solution.py:551
  335.7 5.9 all-to-all-start.5
  342.9 29.2 %all-to-all-done.5 = bf16[8,128,640]{2,1,0:T(8,128)(2,1)} async-done(((bf16[8,128,640]{2,1,0:T(8,128)(2,1)}), bf16[8,128,640]{2,1,0:T(8,128)(2,1)}, u32[]{:S(2)}, u32[]{:S(2)}) %all-to-all-start.5) | async-done | bytes 1310752 | tf_op jit(solution)/shard_map/all_to_all | solution.py:966
  373.8 5.0 multiply_reduce_fusion.1
  381.3 5.7 fusion.19
  401.2 7.5 %convolution_convert_fusion = bf16[3072,768]{1,0:T(8,128)(2,1)} fusion(f32[256,768]{1,0:T(8,128)} %copy-done.19, f32[256,3072]{1,0:T(8,128)} %copy-done.72), kind=kOutput, calls=%fused_computation.1 | convolution fusion | flops 1217593344 | bytes 8650752 | tf_op jit(solution)/shard_map/dot_general | solution.py:746
  429.5 4.9 convolution_convert_fusion.3
  436.9 21.2 %shard_map.345 = (f32[2,128,768]{2,1,0:T(8,128)S(1)}, f32[64,768]{1,0:T(8,128)S(1)}, f32[64,768]{1,0:T(8,128)S(1)}, f32[1,768]{1,0:T(1,128)S(1)}) custom-call(f32[2,128,768]{2,1,0:T(8,128)S(1)} %get-tuple-element.165.input_ref, f32[2,128,768]{2,1,0:T(8,128)S(1)} %get-tuple-element.180.input_ref.grad_ref, ...), custom_call_target="tpu_custom_call" | custom-call | bytes 2362368 | tf_op jit(solution)/shard_map/pallas_call | solution.py:154
  476.2 99.8 %shard_map.346 = (f32[24,2304]{1,0:T(8,128)}, f32[24,3072]{1,0:T(8,128)}, f32[24,768]{1,0:T(8,128)}, f32[24,2304]{1,0:T(8,128)}, f32[96,768]{1,0:T(8,128)}, /*in...) custom-call(bf16[4,2,2,2,24,2560]{5,4,3,2,1,0:T(8,128)(2,1)} %bitcast.264, ...), custom_call_target="tpu_custom_call" | custom-call | bytes 73924608 | tf_op jit(solution)/shard_map/pallas_call | solution.py:419
  (343 shorter events, 145.6 us)
Async XLA Ops:
  7.3 84.3 %copy-start.13 = (bf16[2,128,768]{2,1,0:T(8,128)(2,1)S(1)}, bf16[2,128,768]{2,1,0:T(8,128)(2,1)}, u32[]{:S(2)}) copy-start(bf16[2,128,768]{2,1,0:T(8,128)(2,1)} %param.20) | copy-start | bytes 1179652
  7.3 150.5 %all-gather.3.cloned.1.call-start = ((), (), s32[]{:S(2)}) async-start(), calls=%async_computation.9 | async-start | bytes 16220160 | tf_op jit(solution)/shard_map/all_gather | solution.py:841
  93.2 285.5 %copy-start.47 = (f32[768]{0:T(1024)}, f32[768]{0:T(1024)S(1)}, u32[]{:S(2)}) copy-start(f32[768]{0:T(1024)S(1)} %get-tuple-element.139) | copy-start | bytes 9220
  96.7 3.4 collective-permute-start
  105.8 20.2 %all-to-all-start = ((bf16[8,16,768]{2,1,0:T(8,128)(2,1)}), bf16[8,16,768]{2,1,0:T(8,128)(2,1)S(1)}, u32[]{:S(2)}, u32[]{:S(2)}) async-start(bf16[8,16,768]{2,1,0:T(8,128)(2,1)} %copy_bitcast_fusion.4), calls=%async_computation | async-start | bytes 393216 | tf_op jit(solution)/shard_map/all_to_all | solution.py:192
  112.8 162.6 %all-gather.5.cloned.1.call-start = ((), (), s32[]{:S(2)}) async-start(), calls=%async_computation.10 | async-start | bytes 4866048 | tf_op jit(solution)/shard_map/all_gather | solution.py:905
  159.7 229.4 %copy-start.5 = (f32[256,768]{1,0:T(8,128)}, f32[256,768]{1,0:T(8,128)S(1)}, u32[]{:S(2)}) copy-start(f32[256,768]{1,0:T(8,128)S(1)} %get-tuple-element.208) | copy-start | bytes 2359300
  170.3 208.4 %copy-start.52 = (f32[256]{0:T(256)}, f32[256]{0:T(256)S(1)}, u32[]{:S(2)}) copy-start(f32[256]{0:T(256)S(1)} %broadcast_multiply_fusion.5) | copy-start | bytes 3076
  172.4 78.3 %copy-start.65 = (s32[2]{0:T(128)S(1)}, s32[2]{0:T(128)}, u32[]{:S(2)}) copy-start(s32[2]{0:T(128)} %param.22) | copy-start | bytes 28
  246.5 18.4 %all-to-all-start.3 = ((bf16[8,128,256]{2,1,0:T(8,128)(2,1)}), bf16[8,128,256]{2,1,0:T(8,128)(2,1)}, u32[]{:S(2)}, u32[]{:S(2)}) async-start(bf16[8,128,256]{2,1,0:T(8,128)(2,1)} %bitcast.277), calls=%async_computation.3 | async-start | bytes 1048576 | tf_op jit(solution)/shard_map/all_to_all | solution.py:966
  302.4 20.8 %all-to-all-start.4 = ((bf16[8,128,256]{2,1,0:T(8,128)(2,1)}), bf16[8,128,256]{2,1,0:T(8,128)(2,1)}, u32[]{:S(2)}, u32[]{:S(2)}) async-start(bf16[8,128,256]{2,1,0:T(8,128)(2,1)} %bitcast.267), calls=%async_computation.4 | async-start | bytes 1048576 | tf_op jit(solution)/shard_map/all_to_all | solution.py:961
  335.7 36.5 %all-to-all-start.5 = ((bf16[8,128,640]{2,1,0:T(8,128)(2,1)}), bf16[8,128,640]{2,1,0:T(8,128)(2,1)}, u32[]{:S(2)}, u32[]{:S(2)}) async-start(bf16[8,128,640]{2,1,0:T(8,128)(2,1)} %bitcast.254), calls=%async_computation.5 | async-start | bytes 2621440 | tf_op jit(solution)/shard_map/all_to_all | solution.py:966
  341.6 32.1 %copy-start.61 = (f32[256]{0:T(256)S(1)}, f32[256]{0:T(256)}, u32[]{:S(2)}) copy-start(f32[256]{0:T(256)} %copy-done.60) | copy-start | bytes 3076
  341.6 237.5 %reduce-scatter.2.cloned.1.call-start = ((), (), s32[]{:S(2)}) async-start(), calls=%async_computation.11 | async-start | bytes 10948608 | tf_op jit(solution)/shard_map/reduce_scatter | solution.py:1008
  373.7 13.3 %slice-start.6 = ((s8[15728640]{0:T(1024)(128)(4,1)}), s8[4194304]{0:T(1024)(128)(4,1)S(1)}, s32[]{:S(2)}) async-start(s8[15728640]{0:T(1024)(128)(4,1)} %bitcast.260), calls=%async_computation.18 | async-start | bytes 8388608
  397.1 17.2 %all-to-all-start.6 = ((bf16[8,16,768]{2,1,0:T(8,128)(2,1)}), bf16[8,16,768]{2,1,0:T(8,128)(2,1)}, u32[]{:S(2)}, u32[]{:S(2)}) async-start(bf16[8,16,768]{2,1,0:T(8,128)(2,1)} %copy_bitcast_fusion.1), calls=%async_computation.6 | async-start | bytes 393216 | tf_op jit(solution)/shard_map/all_to_all | solution.py:192
  408.7 15.7 %copy-start.1 = (f32[256,768]{1,0:T(8,128)S(1)}, f32[256,768]{1,0:T(8,128)}, u32[]{:S(2)}) copy-start(f32[256,768]{1,0:T(8,128)} %copy-done) | copy-start | bytes 2359300
  420.2 16.7 %all-to-all-start.7 = ((bf16[8,16,768]{2,1,0:T(8,128)(2,1)}), bf16[8,16,768]{2,1,0:T(8,128)(2,1)S(1)}, u32[]{:S(2)}, u32[]{:S(2)}) async-start(bf16[8,16,768]{2,1,0:T(8,128)(2,1)} %constant_dynamic-update-slice_fusion.13), calls=%async_computation.7 | async-start | bytes 393216 | tf_op jit(solution)/shard_map/all_to_all | solution.py:192
  429.5 28.7 %copy-start.41 = (f32[2,3,768]{2,1,0:T(4,128)S(1)}, f32[2,3,768]{2,1,0:T(4,128)}, u32[]{:S(2)}) copy-start(f32[2,3,768]{2,1,0:T(4,128)} %copy-done.40) | copy-start | bytes 55300
  436.9 21.3 %copy-start.4 = (f32[2,128,2304]{2,1,0:T(8,128)S(1)}, f32[2,128,2304]{2,1,0:T(8,128)}, u32[]{:S(2)}) copy-start(f32[2,128,2304]{2,1,0:T(8,128)} %copy-done.3) | copy-start | bytes 7077892
  461.1 6.2 %collective-permute-start.1 = (f32[2,3,768]{2,1,0:T(4,128)S(1)}, f32[2,3,768]{2,1,0:T(4,128)S(1)}, u32[]{:S(2)}, u32[]{:S(2)}) collective-permute-start(f32[2,3,768]{2,1,0:T(4,128)S(1)} %pad_add_fusion.1), channel_id=1, source_target_pairs={{4,0},{8,4},{12,8},{16,12},{20,16},{24,20},{28,24},{5,1},{9,5},{13... | collective-permute-start | bytes 55304 | tf_op jit(solution)/shard_map/ppermute | solution.py:183
  576.0 14.3 %copy-start.31 = (f32[24,3072]{1,0:T(8,128)S(1)}, f32[24,3072]{1,0:T(8,128)}, u32[]{:S(2)}) copy-start(f32[24,3072]{1,0:T(8,128)} %get-tuple-element.248) | copy-start | bytes 884740
  576.0 15.0 %copy-start.30 = (f32[96,768]{1,0:T(8,128)S(1)}, f32[96,768]{1,0:T(8,128)}, u32[]{:S(2)}) copy-start(f32[96,768]{1,0:T(8,128)} %get-tuple-element.249) | copy-start | bytes 884740
  576.0 15.7 %copy-start.32 = (f32[24,2304]{1,0:T(8,128)S(1)}, f32[24,2304]{1,0:T(8,128)}, u32[]{:S(2)}) copy-start(f32[24,2304]{1,0:T(8,128)} %get-tuple-element.251) | copy-start | bytes 663556
  (73 other events, 302.3 us)
Sparse Core Ops, SparseCore 0:
  13.3 144.4 all-gather.2
  160.7 75.4 all-gather.4
  348.5 154.9 reduce-scatter.1
